TPU v7x, 128 devices: a whole 4x4x4 slice. The times are simulated.
128 devices in a mesh: grp: 4 (over y_hi, core), ctx: 32 (over z, x, y_lo).
Axes of the slice: x: 4, y: 4 (y_hi: 2, y_lo: 2; y = y_hi * 2 + y_lo), z: 4, core: 2. Of those that a mesh axis runs over, the one named last changes fastest.
Arguments:
- cache: bfloat16 [4, 65536, 576], P('grp', 'ctx'), may hold values from -6 to 6
- queries: bfloat16 [4, 4, 4, 128, 576], P(None, 'grp', None, 'ctx'), may hold values from -72 to 72
- new_latent: bfloat16 [4, 4, 4, 576], P(None, 'grp'), may hold values from -12 to 12
- lengths: int32 [4], replicated, may hold values from 32768 to 65536, as said below
- donor: int32 [4], replicated, may hold values from 0 to 3, as said below
- value_up: bfloat16 [128, 512, 128], P('ctx'), may hold values from -2 to 2
- out_proj: bfloat16 [16384, 7168], P('ctx'), may hold values from -0.09375 to 0.09375
Outputs:
- attn_out: bfloat16 [4, 4, 4, 7168], P(None, 'grp', None, 'ctx')
Inputs may be any that keep to these rules, and one draw needn't show every extreme that they name: `lengths`: in every draw some prompt has all 65536 positions valid. `donor`: A slot whose entry is its own index holds a hard prompt; every other entry names such a slot. Slot 3 always holds a hard prompt, and each draw has at least one slot that is not hard.
All inputs are finite; a program needn't handle non-finite values.
Results may differ from a plain program's by a relative error of at most 0.0058.
Values may be sent and summed in bfloat16 or wider, within the bound.
A program may use at most 128 MiB of HBM per device.

v0:
```python
import math

import jax
import jax.numpy as jnp
from jax import lax
from jax.sharding import PartitionSpec as P

HANDOVER = 3


score_scale = 192.0 ** (-0.5)
far_below = -1e30


def from_everyone(x, axis):
    peers = lax.axis_size(axis)
    return lax.all_to_all(jnp.broadcast_to(x[None], (peers, *x.shape)), axis, 0, 0, tiled=True)


def laid_out(pieces, dim):
    lengths = list(pieces.shape[1:])
    lengths[dim] *= pieces.shape[0]
    return jnp.moveaxis(pieces, 0, dim).reshape(lengths)


def collect(x, axis, dim):
    pieces = from_everyone(x, axis)
    return laid_out(pieces, dim)


def side_by_side(arrays, axis, split_dim, concat_dim, along):
    widths = [math.prod(a.shape[along:]) for a in arrays]
    both = jnp.concatenate(
        [a.reshape(*a.shape[:along], w) for a, w in zip(arrays, widths)], axis=along
    )
    whole = lax.all_to_all(both, axis, split_axis=split_dim, concat_axis=concat_dim, tiled=True)
    pieces = jnp.split(whole, [sum(widths[:k]) for k in range(1, len(widths))], axis=along)
    return tuple(
        (b.reshape(*whole.shape[:along], *a.shape[along:]) for a, b in zip(arrays, pieces))
    )


def cut_along(x, dim, peers):
    lengths = x.shape
    pieces = x.reshape(*lengths[:dim], peers, lengths[dim] // peers, *lengths[dim + 1 :])
    return jnp.moveaxis(pieces, dim, 0)


def sent_and_summed(x, axis, dim):
    peers = lax.axis_size(axis)
    pieces = lax.all_to_all(cut_along(x, dim, peers), axis, 0, 0, tiled=True)
    return jnp.sum(pieces, axis=0)


def block_partial(query_rows, cache_rows, valid_mask, latent_width):
    logits = (
        lax.dot_general(
            query_rows, cache_rows, (((1,), (1,)), ((), ())), preferred_element_type=jnp.float32
        )
        * score_scale
    )
    logits = jnp.where(valid_mask[None, :], logits, far_below)
    top_score = jnp.max(logits, axis=1)
    weights = jnp.where(valid_mask[None, :], jnp.exp(logits - top_score[:, None]), 0.0)
    weight_sum = jnp.sum(weights, axis=1)
    partial_out = jnp.dot(
        weights.astype(jnp.bfloat16),
        cache_rows[:, :latent_width],
        preferred_element_type=jnp.float32,
    )
    return (top_score, weight_sum, partial_out)


def combine(earlier, later):
    top_score = jnp.maximum(earlier[0], later[0])
    scale_one = jnp.exp(earlier[0] - top_score)
    scale_two = jnp.exp(later[0] - top_score)
    return (
        top_score,
        earlier[1] * scale_one + later[1] * scale_two,
        earlier[2] * scale_one[..., None] + later[2] * scale_two[..., None],
    )


def serve(query_part, fresh_rows, prompt_rows, limits, value_up, out_proj):
    slot_count, sample_count, owned_heads, key_width = query_part.shape
    latent_width = value_up.shape[1]
    gathered = collect(query_part, "ctx", 2)
    head_count = gathered.shape[2]
    row_count = sample_count * head_count
    local_len = prompt_rows.shape[0]
    positions = lax.axis_index("ctx") * local_len + lax.iota(jnp.int32, local_len)
    top_list, sum_list, part_list = ([], [], [])
    query_rows = gathered[0].reshape(row_count, key_width)
    valid_mask = positions < limits[0]
    found_part = block_partial(query_rows, prompt_rows, valid_mask, latent_width)
    top_list.append(found_part[0].reshape(sample_count, head_count))
    sum_list.append(found_part[1].reshape(sample_count, head_count))
    part_list.append(found_part[2].reshape(sample_count, head_count, latent_width))
    top_score = jnp.stack(top_list)
    weight_sum = jnp.stack(sum_list)
    partial_out = jnp.stack(part_list)
    top_all, sum_all, part_all = side_by_side(
        (top_score[None], weight_sum[None], partial_out[None]), "ctx", 3, 0, 4
    )
    top_score = jnp.max(top_all, axis=0)
    factor = jnp.exp(top_all - top_score[None])
    weight_sum = jnp.sum(sum_all * factor, axis=0)
    partial_out = jnp.sum(part_all * factor[..., None], axis=0)
    query_wide = query_part.astype(jnp.float32)
    fresh_wide = fresh_rows.astype(jnp.float32)
    fresh_logits = jnp.einsum("kshc,tksc->ksht", query_wide, fresh_wide) * score_scale
    fresh_top = jnp.max(fresh_logits, axis=3)
    fresh_weights = jnp.exp(fresh_logits - fresh_top[..., None])
    fresh_sum = jnp.sum(fresh_weights, axis=3)
    fresh_part = jnp.einsum("ksht,tksl->kshl", fresh_weights, fresh_wide[..., :latent_width])
    top_score, weight_sum, partial_out = combine(
        (top_score, weight_sum, partial_out), (fresh_top, fresh_sum, fresh_part)
    )
    attended = (partial_out / weight_sum[..., None]).astype(jnp.bfloat16)
    head_values = jnp.einsum(
        "kshl,hlv->kshv", attended, value_up, preferred_element_type=jnp.float32
    ).astype(jnp.bfloat16)
    term = jnp.dot(
        head_values.reshape(slot_count * sample_count, owned_heads * head_values.shape[3]),
        out_proj,
        preferred_element_type=jnp.float32,
    )
    mixed_out = sent_and_summed(term, "ctx", 1).astype(jnp.bfloat16)
    return mixed_out.reshape(slot_count, sample_count, mixed_out.shape[1])


def body(cache, queries, new_latent, lengths, donor, value_up, out_proj):
    my_group = lax.axis_index("grp")
    group_count = lax.axis_size("grp")
    labels = lax.iota(jnp.int32, group_count)
    own_len = jnp.sum(jnp.where(labels == my_group, lengths, 0))
    own_rows = cache[0]
    results = []
    for step_index in range(HANDOVER):
        results.append(
            serve(
                queries[step_index],
                new_latent[: step_index + 1],
                own_rows,
                own_len[None],
                value_up,
                out_proj,
            )
        )
    source = jnp.sum(jnp.where(labels == my_group, donor, 0))
    shards = lax.all_gather(cache, "grp", axis=0, tiled=True)
    inside = (source >= 0) & (source < shards.shape[0])
    picked = lax.dynamic_index_in_dim(
        shards, jnp.clip(source, 0, shards.shape[0] - 1), 0, keepdims=False
    )
    moved_rows = jnp.where(inside, picked, jnp.zeros_like(own_rows))
    moved_len = jnp.sum(jnp.where(labels == source, lengths, 0))
    step_index = 3
    results.append(
        serve(queries[step_index], new_latent, moved_rows, moved_len[None], value_up, out_proj)
    )
    return jnp.stack(results)


def solution(mesh):
    return jax.shard_map(
        body,
        mesh=mesh,
        in_specs=(
            P("grp", "ctx", None),
            P(None, "grp", None, "ctx", None),
            P(None, "grp", None, None),
            P(),
            P(),
            P("ctx", None, None),
            P("ctx", None),
        ),
        out_specs=P(None, "grp", None, "ctx"),
        check_vma=False,
    )
```

profile of v0, /device:TPU:0, one launch (start us, length us, event | category | flops | bytes accessed | tf_op | source)
XLA Modules:
  0.0 299.9 jit_solution(3964602779020709047)
XLA Ops:
  7.3 0.8 slice_bitcast_fusion.2
  8.1 1.0 broadcast_in_dim.128
  9.1 9.3 %all-to-all-start.3 = ((bf16[32,1,4,4,576]{4,3,2,1,0:T(4,128)(2,1)}), bf16[32,1,4,4,576]{4,3,2,1,0:T(4,128)(2,1)S(1)}, u32[]{:S(2)}, u32[]{:S(2)}) async-start(bf16[32,1,4,4,576]{4,3,2,1,0:T(4,128)(2,1)} %broadcast_in_dim.128), calls=%async_computation.3 | async-start | bytes 1310720 | tf_op jit(solution)/shard_map/all_to_all | solution.py:17
  18.9 13.2 %all-to-all-done.3 = bf16[32,1,4,4,576]{4,3,2,1,0:T(4,128)(2,1)S(1)} async-done(((bf16[32,1,4,4,576]{4,3,2,1,0:T(4,128)(2,1)}), bf16[32,1,4,4,576]{4,3,2,1,0:T(4,128)(2,1)S(1)}, u32[]{:S(2)}, u32[]{:S(2)}) %all-to-all-start.3) | async-done | bytes 589856 | tf_op jit(solution)/shard_map/all_to_all | solution.py:17
  32.1 1.0 broadcast_in_dim.130
  33.1 3.9 %all-to-all-start.6 = ((bf16[32,1,4,4,576]{4,3,2,1,0:T(4,128)(2,1)}), bf16[32,1,4,4,576]{4,3,2,1,0:T(4,128)(2,1)S(1)}, u32[]{:S(2)}, u32[]{:S(2)}) async-start(bf16[32,1,4,4,576]{4,3,2,1,0:T(4,128)(2,1)} %broadcast_in_dim.130), calls=%async_computation.6 | async-start | bytes 1310720 | tf_op jit(solution)/shard_map/all_to_all | solution.py:17
  37.2 13.1 %all-to-all-done.6 = bf16[32,1,4,4,576]{4,3,2,1,0:T(4,128)(2,1)S(1)} async-done(((bf16[32,1,4,4,576]{4,3,2,1,0:T(4,128)(2,1)}), bf16[32,1,4,4,576]{4,3,2,1,0:T(4,128)(2,1)S(1)}, u32[]{:S(2)}, u32[]{:S(2)}) %all-to-all-start.6) | async-done | bytes 589856 | tf_op jit(solution)/shard_map/all_to_all | solution.py:17
  50.3 1.0 broadcast_in_dim.124
  51.3 5.5 %all-to-all-start = ((bf16[32,1,4,4,576]{4,3,2,1,0:T(4,128)(2,1)}), bf16[32,1,4,4,576]{4,3,2,1,0:T(4,128)(2,1)S(1)}, u32[]{:S(2)}, u32[]{:S(2)}) async-start(bf16[32,1,4,4,576]{4,3,2,1,0:T(4,128)(2,1)} %broadcast_in_dim.124), calls=%async_computation | async-start | bytes 1310720 | tf_op jit(solution)/shard_map/all_to_all | solution.py:17
  60.1 10.4 %copy.339 = bf16[512,7168]{0,1:T(8,128)(2,1)} copy(bf16[512,7168]{1,0:T(8,128)(2,1)} %param.13) | data formatting | bytes 14680064 | tf_op args[6]
  70.5 1.3 fusion.98
  73.4 1.2 reshape_squeeze_reshape.13
  75.2 1.0 broadcast_in_dim.134
  76.2 8.8 %all-to-all-start.9 = ((bf16[32,1,4,4,576]{4,3,2,1,0:T(4,128)(2,1)}), bf16[32,1,4,4,576]{4,3,2,1,0:T(4,128)(2,1)S(1)}, u32[]{:S(2)}, u32[]{:S(2)}) async-start(bf16[32,1,4,4,576]{4,3,2,1,0:T(4,128)(2,1)} %broadcast_in_dim.134), calls=%async_computation.9 | async-start | bytes 1310720 | tf_op jit(solution)/shard_map/all_to_all | solution.py:17
  85.5 3.6 %fusion.101 = f32[512,2048]{1,0:T(8,128)S(1)} fusion(bf16[512,576]{1,0:T(8,128)(2,1)S(1)} %reshape_squeeze_reshape.14, bf16[1,2048,576]{1,2,0:T(8,128)(2,1)} %param.7), kind=kOutput, calls=%fused_computation.179 | convolution fusion | flops 1207959552 | bytes 7143424 | tf_op jit(solution)/shard_map/dot_general | solution.py:57
  89.2 2.0 fusion.4
  91.2 3.3 %fusion.9 = (f32[512]{0:T(512)S(1)}, f32[512]{0:T(512)S(1)}, f32[512]{0:T(512)S(1)}, f32[512,2048]{1,0:T(8,128)S(1)}) fusion(f32[512,2048]{1,0:T(8,128)S(1)} %get-tuple-element.34, f32[512]{0:T(512)S(1)} %get-tuple-element.33, pred[2048]{0:T(1024)(128)(4,1)S(1)} %fusion.83, f32[512,2048]{1,0:T(8,128)S(1)} %fusion.101, bf16[512,576]{1,0:T(8,128)(2,1)S(1)} %copy-done.4, ...), kind=kOutput, calls=%fused_computation.21 | convolution fusion | flops 1219492352 | bytes 15542272 | tf_op jit(solution)/shard_map/dot_general | solution.py:57
  94.5 1.3 fusion.20
  96.5 2.4 fusion.11
  99.2 2.2 pad_maximum_fusion.1
  101.4 8.6 %all-to-all-start.4 = ((f32[1,1,4,128,514]{4,2,1,0,3:T(4,128)}), f32[1,1,4,128,514]{4,2,1,0,3:T(4,128)S(1)}, u32[]{:S(2)}, u32[]{:S(2)}) async-start(f32[1,1,4,128,514]{4,2,1,0,3:T(4,128)} %pad_maximum_fusion.1), calls=%async_computation.4 | async-start | bytes 2621440 | tf_op jit(solution)/shard_map/all_to_all | solution.py:36
  110.0 5.1 %fusion.22 = f32[512,512]{1,0:T(8,128)} fusion(f32[512,2048]{1,0:T(8,128)} %copy-done.9, f32[512]{0:T(512)S(1)} %get-tuple-element.33, pred[2048]{0:T(1024)(128)(4,1)S(1)} %fusion.83, bf16[2048,576]{0,1:T(8,128)(2,1)} %bitcast.271), kind=kOutput, calls=%fused_computation.32 | convolution fusion | flops 1078984704 | bytes 7344128 | tf_op jit(solution)/shard_map/dot_general | solution.py:66
  115.4 1.2 reshape_squeeze_reshape.15
  116.7 1.9 copy.328
  118.6 4.2 %fusion.18 = f32[512,512]{1,0:T(8,128)S(1)} fusion(f32[512,2048]{1,0:T(8,128)} %copy-done.1, f32[512]{0:T(512)S(1)} %get-tuple-element.7, pred[2048]{0:T(1024)(128)(4,1)S(1)} %fusion.83, bf16[2048,576]{0,1:T(8,128)(2,1)} %bitcast.272), kind=kOutput, calls=%fused_computation.30 | convolution fusion | flops 1078984704 | bytes 7344128 | tf_op jit(solution)/shard_map/dot_general | solution.py:66
  122.8 1.6 copy.363
  124.6 0.9 copy.327
  125.5 0.9 copy.361
  126.3 3.0 %pad_maximum_fusion = f32[1,1,4,128,514]{4,2,1,0,3:T(4,128)} fusion(f32[1,1,4,128,512]{4,2,1,0,3:T(4,128)S(1)} %copy.328, f32[1,1,4,128,1]{4,2,1,0,3:T(4,128)} %copy.327, f32[1,1,4,128,1]{4,2,1,0,3:T(4,128)S(1)} %copy.326), kind=kLoop, calls=%fused_computation.57 | loop fusion | flops 526336 | bytes 2105344 | tf_op jit(solution)/shard_map/concatenate | solution.py:33
  129.4 3.4 %pad_maximum_fusion.2 = f32[1,1,4,128,514]{4,2,1,0,3:T(4,128)} fusion(f32[1,1,4,128,512]{4,2,1,0,3:T(4,128)} %copy.363, f32[1,1,4,128,1]{4,2,1,0,3:T(4,128)S(1)} %copy.362, f32[1,1,4,128,1]{4,2,1,0,3:T(4,128)} %copy.361), kind=kLoop, calls=%fused_computation.59 | loop fusion | flops 526336 | bytes 2105344 | tf_op jit(solution)/shard_map/concatenate | solution.py:33
  132.7 8.4 %all-to-all-start.7 = ((f32[1,1,4,128,514]{4,2,1,0,3:T(4,128)}), f32[1,1,4,128,514]{4,2,1,0,3:T(4,128)S(1)}, u32[]{:S(2)}, u32[]{:S(2)}) async-start(f32[1,1,4,128,514]{4,2,1,0,3:T(4,128)} %pad_maximum_fusion.2), calls=%async_computation.7 | async-start | bytes 2621440 | tf_op jit(solution)/shard_map/all_to_all | solution.py:36
  141.1 3.8 %copy.344 = f32[1,1,4,32,4,514]{3,4,5,2,1,0:T(4,128)} copy(f32[1,1,4,32,4,514]{5,2,4,3,1,0:T(4,128)S(1)} %bitcast.263) | data formatting | bytes 2105344 | tf_op jit(solution)/shard_map/all_to_all | solution.py:36
  145.8 0.9 fusion.75
  147.8 4.5 %fusion.2 = f32[4,4,512]{1,2,0:T(8,128)S(1)} fusion(f32[32,1,4,4,514]{0,3,4,2,1:T(4,128)} %bitcast.254, f32[32,4,4]{0,2,1:T(4,128)S(1)} %exponential_bitcast_fusion.2), kind=kLoop, calls=%fused_computation.5 | loop fusion | flops 516096 | bytes 1083392 | tf_op jit(solution)/shard_map/reduce_sum | solution.py:109
  152.7 7.0 %all-to-all-done.7 = f32[1,1,4,128,514]{4,2,1,0,3:T(4,128)S(1)} async-done(((f32[1,1,4,128,514]{4,2,1,0,3:T(4,128)}), f32[1,1,4,128,514]{4,2,1,0,3:T(4,128)S(1)}, u32[]{:S(2)}, u32[]{:S(2)}) %all-to-all-start.7) | async-done | bytes 1052704 | tf_op jit(solution)/shard_map/all_to_all | solution.py:36
  159.6 4.3 %all-to-all-start.1 = ((f32[1,1,4,128,514]{4,2,1,0,3:T(4,128)}), f32[1,1,4,128,514]{4,2,1,0,3:T(4,128)S(1)}, u32[]{:S(2)}, u32[]{:S(2)}) async-start(f32[1,1,4,128,514]{4,2,1,0,3:T(4,128)} %pad_maximum_fusion), calls=%async_computation.1 | async-start | bytes 2621440 | tf_op jit(solution)/shard_map/all_to_all | solution.py:36
  164.0 3.8 %copy.364 = f32[1,1,4,32,4,514]{3,4,5,2,1,0:T(4,128)} copy(f32[1,1,4,32,4,514]{5,2,4,3,1,0:T(4,128)S(1)} %bitcast.264) | data formatting | bytes 2105344 | tf_op jit(solution)/shard_map/all_to_all | solution.py:36
  168.6 0.9 fusion.73
  170.6 4.5 %fusion.1 = f32[4,4,512]{1,2,0:T(8,128)S(1)} fusion(f32[32,1,4,4,514]{0,3,4,2,1:T(4,128)} %bitcast.258, f32[32,4,4]{0,2,1:T(4,128)S(1)} %exponential_bitcast_fusion.1), kind=kLoop, calls=%fused_computation.3 | loop fusion | flops 516096 | bytes 1083392 | tf_op jit(solution)/shard_map/reduce_sum | solution.py:109
  175.5 6.6 %all-to-all-done.1 = f32[1,1,4,128,514]{4,2,1,0,3:T(4,128)S(1)} async-done(((f32[1,1,4,128,514]{4,2,1,0,3:T(4,128)}), f32[1,1,4,128,514]{4,2,1,0,3:T(4,128)S(1)}, u32[]{:S(2)}, u32[]{:S(2)}) %all-to-all-start.1) | async-done | bytes 1052704 | tf_op jit(solution)/shard_map/all_to_all | solution.py:36
  182.1 3.7 %copy.329 = f32[1,1,4,32,4,514]{3,4,5,2,1,0:T(4,128)} copy(f32[1,1,4,32,4,514]{5,2,4,3,1,0:T(4,128)S(1)} %bitcast.265) | data formatting | bytes 2105344 | tf_op jit(solution)/shard_map/all_to_all | solution.py:36
  186.7 0.9 fusion.77
  189.1 4.5 %fusion.3 = f32[4,4,512]{1,2,0:T(8,128)S(1)} fusion(f32[32,1,4,4,514]{0,3,4,2,1:T(4,128)} %bitcast.250, f32[32,4,4]{0,2,1:T(4,128)S(1)} %exponential_bitcast_fusion.3), kind=kLoop, calls=%fused_computation.7 | loop fusion | flops 516096 | bytes 1083392 | tf_op jit(solution)/shard_map/reduce_sum | solution.py:109
  193.9 5.8 %convolution_bitcast_fusion.1 = f32[32,4,224]{2,1,0:T(4,128)} fusion(bf16[32,224,512]{2,1,0:T(8,128)(2,1)} %bitcast.243, bf16[4,512,128]{2,1,0:T(8,128)(2,1)S(1)} %copy-done, bf16[4,4,512]{2,1,0:T(4,128)(2,1)S(1)} %fusion.55), kind=kOutput, calls=%fused_computation.62 | convolution fusion | flops 31459328 | bytes 7995392 | tf_op jit(solution)/shard_map/dot_general | solution.py:124
  199.7 1.9 select_bitcast_fusion
  201.6 2.3 fusion.7
  204.0 2.0 fusion.16
  205.9 1.4 fusion.14
  208.4 2.1 pad_maximum_fusion.3
  210.5 4.1 %all-to-all-start.10 = ((f32[1,1,4,128,514]{4,2,1,0,3:T(4,128)}), f32[1,1,4,128,514]{4,2,1,0,3:T(4,128)S(1)}, u32[]{:S(2)}, u32[]{:S(2)}) async-start(f32[1,1,4,128,514]{4,2,1,0,3:T(4,128)} %pad_maximum_fusion.3), calls=%async_computation.10 | async-start | bytes 2621440 | tf_op jit(solution)/shard_map/all_to_all | solution.py:36
  215.0 5.8 %convolution_bitcast_fusion.2 = f32[32,4,224]{2,1,0:T(4,128)} fusion(bf16[32,224,512]{2,1,0:T(8,128)(2,1)} %bitcast.244, bf16[4,512,128]{2,1,0:T(8,128)(2,1)S(1)} %copy-done, bf16[4,4,512]{2,1,0:T(4,128)(2,1)S(1)} %fusion.54), kind=kOutput, calls=%fused_computation.63 | convolution fusion | flops 31459328 | bytes 7995392 | tf_op jit(solution)/shard_map/dot_general | solution.py:124
  220.8 5.8 %convolution_bitcast_fusion.3 = f32[32,4,224]{2,1,0:T(4,128)} fusion(bf16[32,224,512]{2,1,0:T(8,128)(2,1)} %bitcast.245, bf16[4,4,512]{2,0,1:T(4,128)(2,1)S(1)} %copy.338, bf16[4,512,128]{2,1,0:T(8,128)(2,1)S(1)} %copy-done), kind=kOutput, calls=%fused_computation.64 | convolution fusion | flops 31459328 | bytes 7995392 | tf_op jit(solution)/shard_map/dot_general | solution.py:124
  226.7 6.0 %all-to-all-done.10 = f32[1,1,4,128,514]{4,2,1,0,3:T(4,128)S(1)} async-done(((f32[1,1,4,128,514]{4,2,1,0,3:T(4,128)}), f32[1,1,4,128,514]{4,2,1,0,3:T(4,128)S(1)}, u32[]{:S(2)}, u32[]{:S(2)}) %all-to-all-start.10) | async-done | bytes 1052704 | tf_op jit(solution)/shard_map/all_to_all | solution.py:36
  232.7 4.1 %all-to-all-start.8 = ((f32[32,4,224]{2,1,0:T(4,128)}), f32[32,4,224]{2,1,0:T(4,128)S(1)}, u32[]{:S(2)}, u32[]{:S(2)}) async-start(f32[32,4,224]{2,1,0:T(4,128)} %convolution_bitcast_fusion.1), calls=%async_computation.8 | async-start | bytes 262144 | tf_op jit(solution)/shard_map/all_to_all | solution.py:51
  236.8 3.7 %copy.385 = f32[1,1,4,32,4,514]{3,4,5,2,1,0:T(4,128)} copy(f32[1,1,4,32,4,514]{5,2,4,3,1,0:T(4,128)S(1)} %bitcast.266) | data formatting | bytes 2105344 | tf_op jit(solution)/shard_map/all_to_all | solution.py:36
  241.3 0.9 fusion.71
  243.1 4.5 %fusion = f32[4,4,512]{1,2,0:T(8,128)S(1)} fusion(f32[32,1,4,4,514]{0,3,4,2,1:T(4,128)} %bitcast.262, f32[32,4,4]{0,2,1:T(4,128)S(1)} %exponential_bitcast_fusion), kind=kLoop, calls=%fused_computation.1 | loop fusion | flops 516096 | bytes 1083392 | tf_op jit(solution)/shard_map/reduce_sum | solution.py:109
  248.3 8.3 %all-to-all-start.2 = ((f32[32,4,224]{2,1,0:T(4,128)}), f32[32,4,224]{2,1,0:T(4,128)S(1)}, u32[]{:S(2)}, u32[]{:S(2)}) async-start(f32[32,4,224]{2,1,0:T(4,128)} %convolution_bitcast_fusion.3), calls=%async_computation.2 | async-start | bytes 262144 | tf_op jit(solution)/shard_map/all_to_all | solution.py:51
  256.8 8.5 %all-to-all-done.2 = f32[32,4,224]{2,1,0:T(4,128)S(1)} async-done(((f32[32,4,224]{2,1,0:T(4,128)}), f32[32,4,224]{2,1,0:T(4,128)S(1)}, u32[]{:S(2)}, u32[]{:S(2)}) %all-to-all-start.2) | async-done | bytes 114720 | tf_op jit(solution)/shard_map/all_to_all | solution.py:51
  265.3 3.8 %all-to-all-start.5 = ((f32[32,4,224]{2,1,0:T(4,128)}), f32[32,4,224]{2,1,0:T(4,128)S(1)}, u32[]{:S(2)}, u32[]{:S(2)}) async-start(f32[32,4,224]{2,1,0:T(4,128)} %convolution_bitcast_fusion.2), calls=%async_computation.5 | async-start | bytes 262144 | tf_op jit(solution)/shard_map/all_to_all | solution.py:51
  269.1 5.8 %convolution_bitcast_fusion = f32[32,4,224]{2,1,0:T(4,128)} fusion(bf16[32,224,512]{2,1,0:T(8,128)(2,1)} %bitcast.246, bf16[4,512,128]{2,1,0:T(8,128)(2,1)S(1)} %copy-done, bf16[4,4,512]{2,1,0:T(4,128)(2,1)S(1)} %fusion.56), kind=kOutput, calls=%fused_computation.61 | convolution fusion | flops 31459328 | bytes 7995392 | tf_op jit(solution)/shard_map/dot_general | solution.py:124
  275.0 2.9 all-to-all-done.5
  277.9 5.4 %all-to-all-start.11 = ((f32[32,4,224]{2,1,0:T(4,128)}), f32[32,4,224]{2,1,0:T(4,128)S(1)}, u32[]{:S(2)}, u32[]{:S(2)}) async-start(f32[32,4,224]{2,1,0:T(4,128)} %convolution_bitcast_fusion), calls=%async_computation.11 | async-start | bytes 262144 | tf_op jit(solution)/shard_map/all_to_all | solution.py:51
  283.4 8.6 %all-to-all-done.11 = f32[32,4,224]{2,1,0:T(4,128)S(1)} async-done(((f32[32,4,224]{2,1,0:T(4,128)}), f32[32,4,224]{2,1,0:T(4,128)S(1)}, u32[]{:S(2)}, u32[]{:S(2)}) %all-to-all-start.11) | async-done | bytes 114720 | tf_op jit(solution)/shard_map/all_to_all | solution.py:51
  (111 shorter events, 19.2 us)
Async XLA Ops:
  6.5 187.4 %copy-start = (bf16[4,512,128]{2,1,0:T(8,128)(2,1)S(1)}, bf16[4,512,128]{2,1,0:T(8,128)(2,1)}, u32[]{:S(2)}) copy-start(bf16[4,512,128]{2,1,0:T(8,128)(2,1)} %param.12) | copy-start | bytes 1572868
  6.5 11.8 %copy-start.6 = (bf16[4,1,4,4,576]{4,3,2,1,0:T(4,128)(2,1)S(1)}, bf16[4,1,4,4,576]{4,3,2,1,0:T(4,128)(2,1)}, u32[]{:S(2)}) copy-start(bf16[4,1,4,4,576]{4,3,2,1,0:T(4,128)(2,1)} %param.8) | copy-start | bytes 221188
  6.5 11.9 %copy-start.5 = (bf16[4,1,4,576]{3,2,1,0:T(4,128)(2,1)S(1)}, bf16[4,1,4,576]{3,2,1,0:T(4,128)(2,1)}, u32[]{:S(2)}) copy-start(bf16[4,1,4,576]{3,2,1,0:T(4,128)(2,1)} %param.9) | copy-start | bytes 55300
  6.5 50.2 %copy-start.8 = (s32[4]{0:T(128)S(1)}, s32[4]{0:T(128)}, u32[]{:S(2)}) copy-start(s32[4]{0:T(128)} %param.11) | copy-start | bytes 52
  6.5 193.2 %all-gather.2.cloned.1.call-start = ((), (), s32[]{:S(2)}) async-start(), calls=%async_computation.12 | async-start | bytes 11796480 | tf_op jit(solution)/shard_map/all_gather | solution.py:152
  9.1 23.0 %all-to-all-start.3 = ((bf16[32,1,4,4,576]{4,3,2,1,0:T(4,128)(2,1)}), bf16[32,1,4,4,576]{4,3,2,1,0:T(4,128)(2,1)S(1)}, u32[]{:S(2)}, u32[]{:S(2)}) async-start(bf16[32,1,4,4,576]{4,3,2,1,0:T(4,128)(2,1)} %broadcast_in_dim.128), calls=%async_computation.3 | async-start | bytes 1310720 | tf_op jit(solution)/shard_map/all_to_all | solution.py:17
  33.1 17.2 %all-to-all-start.6 = ((bf16[32,1,4,4,576]{4,3,2,1,0:T(4,128)(2,1)}), bf16[32,1,4,4,576]{4,3,2,1,0:T(4,128)(2,1)S(1)}, u32[]{:S(2)}, u32[]{:S(2)}) async-start(bf16[32,1,4,4,576]{4,3,2,1,0:T(4,128)(2,1)} %broadcast_in_dim.130), calls=%async_computation.6 | async-start | bytes 1310720 | tf_op jit(solution)/shard_map/all_to_all | solution.py:17
  51.3 23.8 %all-to-all-start = ((bf16[32,1,4,4,576]{4,3,2,1,0:T(4,128)(2,1)}), bf16[32,1,4,4,576]{4,3,2,1,0:T(4,128)(2,1)S(1)}, u32[]{:S(2)}, u32[]{:S(2)}) async-start(bf16[32,1,4,4,576]{4,3,2,1,0:T(4,128)(2,1)} %broadcast_in_dim.124), calls=%async_computation | async-start | bytes 1310720 | tf_op jit(solution)/shard_map/all_to_all | solution.py:17
  60.1 10.4 %copy-start.7 = (s32[4]{0:T(128)S(1)}, s32[4]{0:T(128)}, u32[]{:S(2)}) copy-start(s32[4]{0:T(128)} %param.10) | copy-start | bytes 52
  76.2 25.3 %all-to-all-start.9 = ((bf16[32,1,4,4,576]{4,3,2,1,0:T(4,128)(2,1)}), bf16[32,1,4,4,576]{4,3,2,1,0:T(4,128)(2,1)S(1)}, u32[]{:S(2)}, u32[]{:S(2)}) async-start(bf16[32,1,4,4,576]{4,3,2,1,0:T(4,128)(2,1)} %broadcast_in_dim.134), calls=%async_computation.9 | async-start | bytes 1310720 | tf_op jit(solution)/shard_map/all_to_all | solution.py:17
  85.5 3.6 %copy-start.2 = (bf16[1,2048,576]{1,2,0:T(8,128)(2,1)S(1)}, bf16[1,2048,576]{1,2,0:T(8,128)(2,1)}, u32[]{:S(2)}) copy-start(bf16[1,2048,576]{1,2,0:T(8,128)(2,1)} %param.7) | copy-start | bytes 7077892
  89.1 7.4 %copy-start.1 = (f32[512,2048]{1,0:T(8,128)}, f32[512,2048]{1,0:T(8,128)S(1)}, u32[]{:S(2)}) copy-start(f32[512,2048]{1,0:T(8,128)S(1)} %fusion.101) | copy-start | bytes 12582916
  89.1 2.0 copy-start.4
  91.2 3.3 %copy-start.9 = (f32[512,2048]{1,0:T(8,128)}, f32[512,2048]{1,0:T(8,128)S(1)}, u32[]{:S(2)}) copy-start(f32[512,2048]{1,0:T(8,128)S(1)} %get-tuple-element.34) | copy-start | bytes 12582916
  101.4 31.3 %all-to-all-start.4 = ((f32[1,1,4,128,514]{4,2,1,0,3:T(4,128)}), f32[1,1,4,128,514]{4,2,1,0,3:T(4,128)S(1)}, u32[]{:S(2)}, u32[]{:S(2)}) async-start(f32[1,1,4,128,514]{4,2,1,0,3:T(4,128)} %pad_maximum_fusion.1), calls=%async_computation.4 | async-start | bytes 2621440 | tf_op jit(solution)/shard_map/all_to_all | solution.py:36
  132.7 26.9 %all-to-all-start.7 = ((f32[1,1,4,128,514]{4,2,1,0,3:T(4,128)}), f32[1,1,4,128,514]{4,2,1,0,3:T(4,128)S(1)}, u32[]{:S(2)}, u32[]{:S(2)}) async-start(f32[1,1,4,128,514]{4,2,1,0,3:T(4,128)} %pad_maximum_fusion.2), calls=%async_computation.7 | async-start | bytes 2621440 | tf_op jit(solution)/shard_map/all_to_all | solution.py:36
  159.6 22.4 %all-to-all-start.1 = ((f32[1,1,4,128,514]{4,2,1,0,3:T(4,128)}), f32[1,1,4,128,514]{4,2,1,0,3:T(4,128)S(1)}, u32[]{:S(2)}, u32[]{:S(2)}) async-start(f32[1,1,4,128,514]{4,2,1,0,3:T(4,128)} %pad_maximum_fusion), calls=%async_computation.1 | async-start | bytes 2621440 | tf_op jit(solution)/shard_map/all_to_all | solution.py:36
  199.7 1.9 copy-start.3
  210.5 22.2 %all-to-all-start.10 = ((f32[1,1,4,128,514]{4,2,1,0,3:T(4,128)}), f32[1,1,4,128,514]{4,2,1,0,3:T(4,128)S(1)}, u32[]{:S(2)}, u32[]{:S(2)}) async-start(f32[1,1,4,128,514]{4,2,1,0,3:T(4,128)} %pad_maximum_fusion.3), calls=%async_computation.10 | async-start | bytes 2621440 | tf_op jit(solution)/shard_map/all_to_all | solution.py:36
  232.7 15.6 %all-to-all-start.8 = ((f32[32,4,224]{2,1,0:T(4,128)}), f32[32,4,224]{2,1,0:T(4,128)S(1)}, u32[]{:S(2)}, u32[]{:S(2)}) async-start(f32[32,4,224]{2,1,0:T(4,128)} %convolution_bitcast_fusion.1), calls=%async_computation.8 | async-start | bytes 262144 | tf_op jit(solution)/shard_map/all_to_all | solution.py:51
  248.3 17.0 %all-to-all-start.2 = ((f32[32,4,224]{2,1,0:T(4,128)}), f32[32,4,224]{2,1,0:T(4,128)S(1)}, u32[]{:S(2)}, u32[]{:S(2)}) async-start(f32[32,4,224]{2,1,0:T(4,128)} %convolution_bitcast_fusion.3), calls=%async_computation.2 | async-start | bytes 262144 | tf_op jit(solution)/shard_map/all_to_all | solution.py:51
  265.3 12.6 %all-to-all-start.5 = ((f32[32,4,224]{2,1,0:T(4,128)}), f32[32,4,224]{2,1,0:T(4,128)S(1)}, u32[]{:S(2)}, u32[]{:S(2)}) async-start(f32[32,4,224]{2,1,0:T(4,128)} %convolution_bitcast_fusion.2), calls=%async_computation.5 | async-start | bytes 262144 | tf_op jit(solution)/shard_map/all_to_all | solution.py:51
  277.9 14.1 %all-to-all-start.11 = ((f32[32,4,224]{2,1,0:T(4,128)}), f32[32,4,224]{2,1,0:T(4,128)S(1)}, u32[]{:S(2)}, u32[]{:S(2)}) async-start(f32[32,4,224]{2,1,0:T(4,128)} %convolution_bitcast_fusion), calls=%async_computation.11 | async-start | bytes 262144 | tf_op jit(solution)/shard_map/all_to_all | solution.py:51
Sparse Core Ops, SparseCore 0:
  9.0 94.5 all-gather.1
where the time goes:
time: 306 us; the launch traced here: 300 us
  starting transfers between devices  74.4 us (24%)
  waiting for transfers between devices  66.5 us (22%)
  other arithmetic  48.6 us (16%)
  matrix products  48.3 us (16%)
  local copies, waits for them, and re-layouts  45.8 us (15%)
  between operations  16.3 us (5%)
    all_to_all x4, starting transfers between devices, from_everyone(): lax.all_to_all(jnp.broadcast_to(x[None], (peers, *x.shape)), axis, 0, 0,...  27.4 us
    all_to_all x4, waiting for transfers between devices, from_everyone(): lax.all_to_all(jnp.broadcast_to(x[None], (peers, *x.shape)), axis, 0, 0,...  26.3 us
    all_to_all x4, starting transfers between devices, side_by_side(): lax.all_to_all(both, axis, split_axis=split_dim, concat_axis=concat_dim,...  25.4 us
    dot_general x4, matrix products, serve(): jnp.dot(head_values.reshape(slot_count * sample_count, owned_heads * head...  23.3 us
    all_to_all x4, starting transfers between devices, sent_and_summed(): pieces = lax.all_to_all(cut_along(x, dim, peers), axis, 0, 0, tiled=True)  21.6 us
    all_to_all x4, waiting for transfers between devices, sent_and_summed(): pieces = lax.all_to_all(cut_along(x, dim, peers), axis, 0, 0, tiled=True)  20 us
    all_to_all x4, waiting for transfers between devices, side_by_side(): lax.all_to_all(both, axis, split_axis=split_dim, concat_axis=concat_dim,...  19.6 us
    reduce_sum x4, other arithmetic, serve(): partial_out = jnp.sum(part_all * factor[..., None], axis=0)  18 us
  transfers between devices with their start and end apart: 13, of which 8 were waited for; matrix products, arithmetic and copies ran while one was open for 44% of the time, Pallas kernels for 0%

commit v1 on v0

v1 whole, which is shorter than its diff:
```python
import functools

import jax
import jax.numpy as jnp
from jax import lax
from jax.experimental import pallas as pl
from jax.experimental.pallas import tpu as pltpu
from jax.sharding import PartitionSpec as P

MESH = pl.DeviceIdType.MESH
LATENT = 512
KEYW = 576
CTX = 2048
ROWS = 16
UNIT = 256
NPART = 5
OUTW = 224
NPEER = 32
SCALE2 = (192.0 ** -0.5) * 1.4426950408889634
LOW = -1e30
FLOOR = -1e29
BF = jnp.bfloat16
F32 = jnp.float32


def rounded(v):
    return v.astype(BF).astype(F32)


def lanes_of(shape):
    return lax.broadcasted_iota(jnp.int32, shape, 1)


def put(tile, lane, j, m, s):
    hi = rounded(s)
    tile = jnp.where(lane == j, m, tile)
    tile = jnp.where(lane == 16 + j, hi, tile)
    return jnp.where(lane == 32 + j, s - hi, tile)


def take(tile, j):
    return tile[:, j:j + 1], tile[:, 16 + j:17 + j] + tile[:, 32 + j:33 + j]


def merged(ma, sa, oa, mb, sb, ob):
    top = jnp.maximum(ma, mb)
    fa = jnp.exp2(ma - top)
    fb = jnp.exp2(mb - top)
    return top, sa * fa + sb * fb, oa * fa + ob * fb


def kernel(lim_ref, sel_ref, q_ref, nl_ref, cache_ref, vu_ref, op_ref, out_ref,
           cbuf, qbuf, obuf, stat, ra, ras, rc, rcs, rb, rbs, rd, rds, ry, rys, rf, rfs,
           sbuf, rbuf, opv, vuv, scr, fo, fm, fs,
           csem, gsend, grecv, rsend, rrecv, xsend, xrecv, ysend, yrecv):
    g = lax.axis_index("grp")
    c = lax.axis_index("ctx")
    h = g // 2
    k = g % 2
    z = c // 8
    x = (c // 2) % 4
    y = c % 2
    other = c + 1 - 2 * y

    def nbr(p, axis_b, delta):
        along_z = (p == 0) != axis_b
        if along_z:
            return (g, ((z + delta + 4) % 4) * 8 + x * 2 + y)
        return (g, z * 8 + ((x + delta + 4) % 4) * 2 + y)

    def rdma(src, dst, ss, rs, dev):
        return pltpu.make_async_remote_copy(src_ref=src, dst_ref=dst, send_sem=ss, recv_sem=rs,
                                            device_id=dev, device_id_type=MESH)

    barrier = pltpu.get_barrier_semaphore()

    def greet(i, carry):
        pl.semaphore_signal(barrier, inc=1, device_id=(g, (c + i) % NPEER), device_id_type=MESH)
        return carry

    lax.fori_loop(1, NPEER, greet, 0)
    for dg in range(1, 4):
        for dc in (c, other):
            pl.semaphore_signal(barrier, inc=1, device_id=((g + dg) % 4, dc), device_id_type=MESH)

    own_copy = pltpu.make_async_copy(cache_ref, cbuf.at[0], csem.at[0])
    own_copy.start()
    op_copy = pltpu.make_async_copy(op_ref, opv, csem.at[1])
    op_copy.start()
    vu_copy = pltpu.make_async_copy(vu_ref, vuv, csem.at[2])
    vu_copy.start()
    for t in range(3):
        qbuf[0, t, 0, 0] = q_ref[t]

    pl.semaphore_wait(barrier, NPEER - 1 + 6)

    def ycopy(t):
        return rdma(q_ref.at[t], qbuf.at[1, t, 0, 0], gsend.at[t], grecv.at[t], (g, other))

    for t in range(3):
        ycopy(t).start()

    def slot_copy(s, i, dev):
        return rdma(q_ref.at[3], qbuf.at[s % 2, 3 + s // 2, 0, 0], gsend.at[3 + i], grecv.at[3 + s], dev)

    for hh in range(2):
        for yy in range(2):
            dev = (2 * hh + y, z * 8 + x * 2 + yy)
            mine = (2 * hh + y == g) & (y == yy)

            @pl.when(jnp.logical_not(mine))
            def _():
                slot_copy(g, 2 * hh + yy, dev).start()

    @pl.when(y == k)
    def _():
        qbuf[g % 2, 3 + g // 2, 0, 0] = q_ref[3]

    swap = rdma(cache_ref, cbuf.at[1], csem.at[3], csem.at[4], (g + 1 - 2 * k, c))
    swap.start()

    lane_k = lax.broadcasted_iota(jnp.int32, (ROWS, ROWS), 1)
    row_s = lax.broadcasted_iota(jnp.int32, (ROWS, ROWS), 0) // 4
    nl = nl_ref[...]
    for t in range(4):
        logits = lax.dot_general(q_ref[t], nl, (((1,), (1,)), ((), ())), preferred_element_type=F32)
        ok = (lane_k % 4 == row_s) & (lane_k // 4 <= t)
        logits = jnp.where(ok, logits * SCALE2, LOW)
        top = jnp.max(logits, axis=1, keepdims=True)
        w = jnp.where(ok, jnp.exp2(logits - top), 0.0)
        whi = w.astype(BF)
        wlo = (w - whi.astype(F32)).astype(BF)
        val = nl[:, :LATENT]
        fo[t] = (jnp.dot(whi, val, preferred_element_type=F32)
                 + jnp.dot(wlo, val, preferred_element_type=F32))
        fm[t] = jnp.broadcast_to(top, (ROWS, 128))
        fs[t] = jnp.broadcast_to(jnp.sum(w, axis=1, keepdims=True), (ROWS, 128))

    def sems(p, t, i):
        n = (p * NPART + t) * 8 + i
        return gsend.at[8 + n], grecv.at[8 + n]

    def g1(p, t, sign):
        return rdma(qbuf.at[p, t, 0, 0], qbuf.at[p, t, 0, 3 if sign > 0 else 1],
                    *sems(p, t, 0 if sign > 0 else 1), nbr(p, True, sign))

    def g1f(p, t):
        sign = 1 if t % 2 == 0 else -1
        return rdma(qbuf.at[p, t, 0, 3 if sign > 0 else 1], qbuf.at[p, t, 0, 2],
                    *sems(p, t, 2), nbr(p, True, sign))

    def g2(p, t, sign):
        return rdma(qbuf.at[p, t, 0], qbuf.at[p, t, 3 if sign > 0 else 1],
                    *sems(p, t, 3 if sign > 0 else 4), nbr(p, False, sign))

    def g2f(p, t, sign):
        half = pl.ds(0, 2) if sign > 0 else pl.ds(2, 2)
        return rdma(qbuf.at[p, t, 3 if sign > 0 else 1, half], qbuf.at[p, t, 2, half],
                    *sems(p, t, 5 if sign > 0 else 6), nbr(p, False, sign))

    units = [(p, t) for t in range(NPART) for p in range(2)]
    for p, t in units:
        if t < 3:
            if p == 1:
                ycopy(t).wait_recv()
        else:
            s = (t - 3) * 2 + p
            mine = (g == s) & (y == k)

            @pl.when(jnp.logical_not(mine))
            def _():
                slot_copy(s, 0, (g, c)).wait_recv()
        g1(p, t, 1).start()
        g1(p, t, -1).start()
    for p, t in units:
        first, second = (1, -1) if t % 2 == 0 else (-1, 1)
        g1(p, t, first).wait_recv()
        g1f(p, t).start()
    for p, t in units:
        second = -1 if t % 2 == 0 else 1
        g1(p, t, second).wait_recv()
        g1f(p, t).wait_recv()
        g2(p, t, 1).start()
        g2(p, t, -1).start()
    for p, t in units:
        for sign in (1, -1):
            g2(p, t, sign).wait_recv()
            g2f(p, t, sign).start()
    for p, t in units:
        for sign in (1, -1):
            g2f(p, t, sign).wait_recv()

    own_copy.wait()
    swap.wait()

    lane = lanes_of((ROWS, 128))
    nj = 4
    wj = CTX // nj

    def attend(u, carry):
        p = u % 2
        t = u // 2
        limit = lim_ref[u]
        sel = sel_ref[u]
        q = qbuf[p, t].reshape(UNIT, KEYW)
        top = jnp.full((UNIT, 1), FLOOR, F32)
        for j in range(nj):
            pos = lax.broadcasted_iota(jnp.int32, (1, wj), 1) + j * wj
            bias = jnp.where(pos < limit, 0.0, LOW)
            sc = jnp.dot(q, cbuf[sel, :, j * wj:(j + 1) * wj], preferred_element_type=F32) * SCALE2 + bias
            scr[:, j * wj:(j + 1) * wj] = sc
            top = jnp.maximum(top, jnp.max(sc, axis=1, keepdims=True))
        top = rounded(top)
        total = jnp.zeros((UNIT, 1), F32)
        acc = jnp.zeros((UNIT, LATENT), F32)
        for j in range(nj):
            w = jnp.exp2(scr[:, j * wj:(j + 1) * wj] - top)
            total = total + jnp.sum(w, axis=1, keepdims=True)
            acc = acc + lax.dot_general(w.astype(BF), cbuf[sel, :LATENT, j * wj:(j + 1) * wj],
                                        (((1,), (1,)), ((), ())), preferred_element_type=F32)
        obuf[p, t] = acc.astype(BF).reshape(4, 4, ROWS, LATENT)
        tile = jnp.zeros((ROWS, 128), F32)
        for j in range(16):
            tile = put(tile, lane, j, top[j * ROWS:(j + 1) * ROWS], total[j * ROWS:(j + 1) * ROWS])
        stat[p, t] = tile.astype(BF)
        return carry

    lax.fori_loop(0, 2 * NPART, attend, 0)

    def rsem(p, t, i):
        n = (p * NPART + t) * 16 + i
        return rsend.at[n], rrecv.at[n]

    def fold(p, t, a, b, tile_in, j_in, data_in, tile):
        j = a * 4 + b
        ma, sa = take(tile, j)
        mb, sb = take(tile_in, j_in)
        m, s, o = merged(ma, sa, obuf[p, t, a, b].astype(F32), mb, sb, data_in.astype(F32))
        obuf[p, t, a, b] = o.astype(BF)
        return put(tile, lane, j, m, s)

    def a1(p, t, sign):
        i = 0 if sign > 0 else 1
        half = pl.ds(0, 2) if sign > 0 else pl.ds(2, 2)
        dev = nbr(p, False, sign)
        return (rdma(obuf.at[p, t, 2, half], ra.at[p, t, i], *rsem(p, t, i), dev),
                rdma(stat.at[p, t], ras.at[p, t, i], *rsem(p, t, 2 + i), dev))

    def a2(p, t, sign):
        i = 0 if sign > 0 else 1
        dev = nbr(p, False, sign)
        return (rdma(obuf.at[p, t, 1 if sign > 0 else 3], rc.at[p, t, i], *rsem(p, t, 4 + i), dev),
                rdma(stat.at[p, t], rcs.at[p, t, i], *rsem(p, t, 6 + i), dev))

    def b1(p, t):
        sign = 1 if t % 2 == 0 else -1
        dev = nbr(p, True, sign)
        return (rdma(obuf.at[p, t, 0, 2], rb.at[p, t], *rsem(p, t, 8), dev),
                rdma(stat.at[p, t], rbs.at[p, t], *rsem(p, t, 9), dev))

    def b2(p, t, sign):
        i = 0 if sign > 0 else 1
        dev = nbr(p, True, sign)
        return (rdma(obuf.at[p, t, 0, 1 if sign > 0 else 3], rd.at[p, t, i], *rsem(p, t, 10 + i), dev),
                rdma(stat.at[p, t], rds.at[p, t, i], *rsem(p, t, 12 + i), dev))

    def start(pair):
        for cp in pair:
            cp.start()

    def got(pair):
        for cp in pair:
            cp.wait_recv()

    def gone(pair):
        for cp in pair:
            cp.wait_send()

    for p, t in units:
        start(a1(p, t, 1))
        start(a1(p, t, -1))
    for p, t in units:
        for sign in (1, -1):
            got(a1(p, t, sign))
            gone(a1(p, t, sign))
        tile = stat[p, t].astype(F32)
        for i in range(2):
            tin = ras[p, t, i].astype(F32)
            for b in range(2):
                bb = 2 * i + b
                tile = fold(p, t, 1 if i == 0 else 3, bb, tin, 8 + bb, ra[p, t, i, b], tile)
        stat[p, t] = tile.astype(BF)
        start(a2(p, t, 1))
        start(a2(p, t, -1))
    for p, t in units:
        for sign in (1, -1):
            got(a2(p, t, sign))
            gone(a2(p, t, sign))
        tile = stat[p, t].astype(F32)
        for i in range(2):
            tin = rcs[p, t, i].astype(F32)
            for b in range(4):
                tile = fold(p, t, 0, b, tin, (4 if i == 0 else 12) + b, rc[p, t, i, b], tile)
        stat[p, t] = tile.astype(BF)
        start(b1(p, t))
    for p, t in units:
        got(b1(p, t))
        gone(b1(p, t))
        tile = stat[p, t].astype(F32)
        tile = fold(p, t, 0, 1 if t % 2 == 0 else 3, rbs[p, t].astype(F32), 2, rb[p, t], tile)
        stat[p, t] = tile.astype(BF)
        start(b2(p, t, 1))
        start(b2(p, t, -1))

    def yback(t):
        return (rdma(obuf.at[1, t, 0, 0], ry.at[t], ysend.at[2 * t], yrecv.at[2 * t], (g, other)),
                rdma(stat.at[1, t], rys.at[t], ysend.at[2 * t + 1], yrecv.at[2 * t + 1], (g, other)))

    def sback(s, src):
        dev = (s, z * 8 + x * 2 + k)
        return (rdma(obuf.at[s % 2, 3 + s // 2, 0, 0], rf.at[src], ysend.at[6 + 2 * s], yrecv.at[6 + 2 * src], dev),
                rdma(stat.at[s % 2, 3 + s // 2], rfs.at[src], ysend.at[7 + 2 * s], yrecv.at[7 + 2 * src], dev))

    for p, t in units:
        for sign in (1, -1):
            got(b2(p, t, sign))
            gone(b2(p, t, sign))
        tile = stat[p, t].astype(F32)
        for i in range(2):
            tile = fold(p, t, 0, 0, rds[p, t, i].astype(F32), 1 if i == 0 else 3, rd[p, t, i], tile)
        stat[p, t] = tile.astype(BF)
        if t < 3:
            if p == 1:
                start(yback(t))
        else:
            s = (t - 3) * 2 + p
            mine = (g == s) & (y == k)

            @pl.when(jnp.logical_not(mine))
            def _():
                start(sback(s, 2 * h + y))

            @pl.when(mine)
            def _():
                rf[2 * h + y] = obuf[p, t, 0, 0]
                rfs[2 * h + y] = stat[p, t]

    att = []

    def finish(t, m, s, o):
        m, s, o = merged(m, s, o, fm[t][:, :1], fs[t][:, :1], fo[t])
        att.append((o / s).astype(BF))

    for t in range(3):
        got(yback(t))
        m, s = take(stat[0, t].astype(F32), 0)
        mb, sb = take(rys[t].astype(F32), 0)
        m, s, o = merged(m, s, obuf[0, t, 0, 0].astype(F32), mb, sb, ry[t].astype(F32))
        finish(t, m, s, o)
    m = s = o = None
    for src in range(4):
        mine = (y == k) & (src == 2 * h + y)

        @pl.when(jnp.logical_not(mine))
        def _():
            got(sback(0, src))
        mb, sb = take(rfs[src].astype(F32), 0)
        ob = rf[src].astype(F32)
        if src == 0:
            m, s, o = mb, sb, ob
        else:
            m, s, o = merged(m, s, o, mb, sb, ob)
    finish(3, m, s, o)

    attended = jnp.concatenate(att, axis=0)
    vu_copy.wait()
    op_copy.wait()
    row_head = lax.broadcasted_iota(jnp.int32, (64, 128), 0) % 4
    pieces = []
    for head in range(4):
        hv = jnp.dot(attended, vuv[head], preferred_element_type=F32)
        pieces.append(jnp.where(row_head == head, hv, 0.0).astype(BF))
    spread = jnp.concatenate(pieces, axis=1)
    pick = (lax.broadcasted_iota(jnp.int32, (ROWS, 64), 1) // 4
            == lax.broadcasted_iota(jnp.int32, (ROWS, 64), 0))
    joined = jnp.dot(jnp.where(pick, 1.0, 0.0).astype(BF), spread, preferred_element_type=F32).astype(BF)

    def outc(dest, rel):
        return rdma(sbuf.at[dest], rbuf.at[rel], xsend.at[dest], xrecv.at[rel], (g, dest))

    width = 8 * OUTW
    for blk in range(4):
        term = jnp.dot(joined, opv[:, blk * width:(blk + 1) * width], preferred_element_type=F32)
        for i in range(8):
            sbuf[blk * 8 + i, :, :OUTW] = term[:, i * OUTW:(i + 1) * OUTW].astype(BF)

    def send_out(i, carry):
        outc((c + i) % NPEER, (NPEER - i) % NPEER).start()
        return carry

    lax.fori_loop(1, NPEER, send_out, 0)

    for t in range(3):
        ycopy(t).wait_send()
        gone(yback(t))
    for hh in range(2):
        for yy in range(2):
            mine = (2 * hh + y == g) & (y == yy)

            @pl.when(jnp.logical_not(mine))
            def _():
                slot_copy(g, 2 * hh + yy, (g, c)).wait_send()
    for s in range(4):
        mine = (g == s) & (y == k)

        @pl.when(jnp.logical_not(mine))
        def _():
            gone(sback(s, 0))
    for p, t in units:
        g1f(p, t).wait_send()
        for sign in (1, -1):
            g1(p, t, sign).wait_send()
            g2(p, t, sign).wait_send()
            g2f(p, t, sign).wait_send()

    res = sbuf[c][:, :OUTW].astype(F32)
    for rel in range(1, NPEER):
        pltpu.make_async_remote_copy(src_ref=sbuf.at[0], dst_ref=rbuf.at[rel], send_sem=xsend.at[0],
                                     recv_sem=xrecv.at[rel], device_id=(g, c), device_id_type=MESH).wait_recv()
        res = res + rbuf[rel][:, :OUTW].astype(F32)
    out_ref[...] = res.astype(BF)

    def sent_out(i, carry):
        outc((c + i) % NPEER, (NPEER - i) % NPEER).wait_send()
        return carry

    lax.fori_loop(1, NPEER, sent_out, 0)


def body(cache, queries, new_latent, lengths, donor, value_up, out_proj):
    g = lax.axis_index("grp")
    c = lax.axis_index("ctx")
    start = c * CTX
    own = jnp.sum(jnp.where(jnp.arange(4, dtype=jnp.int32) == g, lengths, 0)) - start
    src_len = jnp.sum(jnp.where(donor[:, None] == jnp.arange(4, dtype=jnp.int32)[None], lengths[None], 0), axis=1)
    slot_lim = jnp.where(donor // 2 == g // 2, src_len - start, 0)
    slot_sel = (donor % 2 != g % 2).astype(jnp.int32)
    limits = jnp.concatenate([jnp.broadcast_to(own, (6,)), slot_lim]).astype(jnp.int32)
    select = jnp.concatenate([jnp.zeros((6,), jnp.int32), slot_sel])
    keys = jnp.swapaxes(cache[0], 0, 1)
    q = queries.reshape(4, ROWS, KEYW)
    nl = new_latent.reshape(ROWS, KEYW)
    VM, SM, ANY = pltpu.VMEM, pltpu.SMEM, pl.ANY
    U = (2, NPART)
    dma = pltpu.SemaphoreType.DMA
    out = pl.pallas_call(
        kernel,
        out_shape=jax.ShapeDtypeStruct((ROWS, OUTW), BF),
        in_specs=[pl.BlockSpec(memory_space=m) for m in (SM, SM, VM, VM, ANY, ANY, ANY)],
        out_specs=pl.BlockSpec(memory_space=VM),
        scratch_shapes=[
            VM((2, KEYW, CTX), BF),
            VM(U + (4, 4, ROWS, KEYW), BF),
            VM(U + (4, 4, ROWS, LATENT), BF),
            VM(U + (ROWS, 128), BF),
            VM(U + (2, 2, ROWS, LATENT), BF), VM(U + (2, ROWS, 128), BF),
            VM(U + (2, 4, ROWS, LATENT), BF), VM(U + (2, ROWS, 128), BF),
            VM(U + (ROWS, LATENT), BF), VM(U + (ROWS, 128), BF),
            VM(U + (2, ROWS, LATENT), BF), VM(U + (2, ROWS, 128), BF),
            VM((3, ROWS, LATENT), BF), VM((3, ROWS, 128), BF),
            VM((4, ROWS, LATENT), BF), VM((4, ROWS, 128), BF),
            VM((NPEER, ROWS, 256), BF), VM((NPEER, ROWS, 256), BF),
            VM((512, 7168), BF), VM((4, LATENT, 128), BF),
            VM((UNIT, CTX), F32),
            VM((4, ROWS, LATENT), F32), VM((4, ROWS, 128), F32), VM((4, ROWS, 128), F32),
            dma((5,)), dma((88,)), dma((88,)), dma((160,)), dma((160,)),
            dma((NPEER,)), dma((NPEER,)), dma((16,)), dma((16,)),
        ],
        compiler_params=pltpu.CompilerParams(collective_id=0, has_side_effects=True,
                                             vmem_limit_bytes=56 * 1024 * 1024),
        name="mla_step",
    )(limits, select, q, nl, keys, value_up, out_proj)
    return out.reshape(4, 1, 4, OUTW)


def solution(mesh):
    return jax.shard_map(
        body,
        mesh=mesh,
        in_specs=(
            P("grp", "ctx", None),
            P(None, "grp", None, "ctx", None),
            P(None, "grp", None, None),
            P(),
            P(),
            P("ctx", None, None),
            P("ctx", None),
        ),
        out_specs=P(None, "grp", None, "ctx"),
        check_vma=False,
    )
```

time: 306 us -> 128 us (0.42); the launches traced: 300 us -> 127 us
  Pallas kernels: 0 us -> 117 us
  starting transfers between devices: 74.4 us -> 0 us
  waiting for transfers between devices: 66.5 us -> 0 us
  matrix products: 48.3 us -> 0 us
  other arithmetic: 48.6 us -> 4.06 us
  local copies, waits for them, and re-layouts: 45.8 us -> 4.79 us
  between operations: 16.3 us -> 0.67 us
    pallas_call x0 -> x1, Pallas kernels: none -> 117 us  [body(): pl.pallas_call(kernel, out_shape=jax.ShapeDtypeStruct((ROWS, OUTW), BF),...]
    all_to_all x12 -> x0, starting transfers between devices: 74.4 us -> none  [the longest x4 27.4 us: from_everyone(): lax.all_to_all(jnp.broadcast_to(x[None], (peers, *x.shape)), axis, 0, 0,...]
    all_to_all x12 -> x0, waiting for transfers between devices: 65.8 us -> none  [the longest x4 26.3 us: from_everyone(): lax.all_to_all(jnp.broadcast_to(x[None], (peers, *x.shape)), axis, 0, 0,...]
    dot_general x19 -> x0, matrix products: 48.3 us -> none  [the longest x4 23.3 us: serve(): jnp.dot(head_values.reshape(slot_count * sample_count, owned_heads * head...]
    reduce_sum x19 -> x2, other arithmetic: 27.5 us -> 2.14 us  [the longest x1 1.29 us: body(): jnp.sum(jnp.where(jnp.arange(4, dtype=jnp.int32) == g, lengths, 0)) - start]
    all_to_all x4 -> x0, local copies, waits for them, and re-layouts: 15 us -> none  [side_by_side(): lax.all_to_all(both, axis, split_axis=split_dim, concat_axis=concat_dim,...]
    unnamed x25 -> x0, local copies, waits for them, and re-layouts: 10.9 us -> none
    another operation x17 -> x0, local copies, waits for them, and re-layouts: 10.7 us -> none  [the longest x4 4.9 us: serve(): partial_out[None]]
  transfers between devices with their start and end apart: 13 -> 0, of which waited for: 8 -> 0; matrix products, arithmetic and copies ran while one was open for 44% -> 0% of each run, Pallas kernels for 0% -> 0%
where the time goes in v1:
time: 128 us; the launch traced here: 127 us
  Pallas kernels  117 us (91%)
  local copies, waits for them, and re-layouts  4.79 us (4%)
  other arithmetic  4.06 us (3%)
    pallas_call x1, Pallas kernels, body(): pl.pallas_call(kernel, out_shape=jax.ShapeDtypeStruct((ROWS, OUTW), BF),...  117 us

profile of v1, /device:TPU:0, one launch (start us, length us, event | category | flops | bytes accessed | tf_op | source)
XLA Modules:
  0.0 126.9 jit_solution(15072284934287813122)
XLA Ops:
  0.0 1.3 %fusion = s32[]{:T(128)} fusion(s32[4]{0:T(128)} %param.10, s32[]{:T(128)S(6)} %axis_index.23), kind=kLoop, calls=%fused_computation.10 | loop fusion | flops 11 | bytes 24 | tf_op jit(solution)/shard_map/reduce_sum | solution.py:444
  1.9 0.7 fusion.1
  2.6 0.6 pad_convert_fusion.sel_ref
  3.2 0.9 select_reduce_fusion
  4.0 0.7 compare_select_fusion.1
  4.7 0.6 concatenate.8.lim_ref
  5.3 1.4 %reshape.12.nl_ref = bf16[16,576]{1,0:T(8,128)(2,1)} reshape(bf16[4,1,4,576]{3,2,1,0:T(4,128)(2,1)} %param.9) | data formatting | bytes 36864 | tf_op jit(solution)/shard_map/reshape | solution.py:452
  6.7 1.5 %reshape.11.q_ref = bf16[4,16,576]{2,1,0:T(8,128)(2,1)} reshape(bf16[4,1,4,4,576]{4,3,2,1,0:T(4,128)(2,1)} %param.8) | data formatting | bytes 147456 | tf_op jit(solution)/shard_map/reshape | solution.py:451
  8.2 117.4 %mla_step.1 = bf16[16,224]{1,0:T(8,128)(2,1)} custom-call(s32[10]{0:T(128)} %concatenate.8.lim_ref, s32[10]{0:T(128)} %pad_convert_fusion.sel_ref, bf16[4,16,576]{2,1,0:T(8,128)(2,1)} %reshape.11.q_ref, bf16[16,576]{1,0:T(8,128)(2,1)} %reshape.12.nl_ref, bf16[576,2048]{1,0:T(8,128)(2,1)} %bitcast.4, bf16[4,512,128]{2,1,0:T(8,128)(2,1)} %vu_ref.1, ...), custom_call_target="tpu_custom_call" | custom-call | tf_op jit(solution)/shard_map/mla_step/pallas_call | solution.py:456
  125.6 1.3 %reshape.13 = bf16[4,1,4,224]{3,2,0,1:T(4,128)(2,1)} reshape(bf16[16,224]{1,0:T(8,128)(2,1)} %mla_step.1) | data formatting | bytes 14336 | tf_op jit(solution)/shard_map/reshape | solution.py:483

commit v2 on v1

v2 whole, which is shorter than its diff:
```python
import functools

import jax
import jax.numpy as jnp
from jax import lax
from jax.experimental import pallas as pl
from jax.experimental.pallas import tpu as pltpu
from jax.sharding import PartitionSpec as P

MESH = pl.DeviceIdType.MESH
LATENT = 512
KEYW = 576
CTX = 2048
ROWS = 16
UNIT = 256
NPART = 5
OUTW = 224
NPEER = 32
SCALE2 = (192.0 ** -0.5) * 1.4426950408889634
LOW = -1e30
FLOOR = -1e29
BF = jnp.bfloat16
F32 = jnp.float32


def rounded(v):
    return v.astype(BF).astype(F32)


def lanes_of(shape):
    return lax.broadcasted_iota(jnp.int32, shape, 1)


def stats(tile):
    t = tile.astype(F32)
    return t, pltpu.roll(t, 124, 1) + pltpu.roll(t, 120, 1)


def combine(parts):
    top = parts[0][0]
    for t, _ in parts[1:]:
        top = jnp.maximum(top, t)
    factors = [jnp.exp2(t - top) for t, _ in parts]
    total = factors[0] * parts[0][1]
    for f, (_, v) in zip(factors[1:], parts[1:]):
        total = total + f * v
    return top, total, factors


def packed(top, total):
    lane = lanes_of(top.shape)
    hi = rounded(total)
    lo = total - hi
    return jnp.where(lane < 4, top, jnp.where(lane < 8, pltpu.roll(hi, 4, 1), pltpu.roll(lo, 8, 1))).astype(BF)


def kernel(len_ref, don_ref, q_ref, nl_ref, cache_ref, vu_ref, op_ref, out_ref,
           cbuf, qown, qbuf, obuf, stat, ra, ras, rc, rcs, rd, rds, rf, rfs,
           sbuf, rbuf, opv, vuv, scr, fo, fst,
           csem, hsend, hrecv, gsend, grecv, rsend, rrecv, xsend, xrecv, dsend, drecv, fsend, frecv):
    g = lax.axis_index("grp")
    c = lax.axis_index("ctx")
    h = g // 2
    k = g % 2
    z = c // 8
    x = (c // 2) % 4
    y = c % 2
    other = c + 1 - 2 * y

    def at(dz, dx, yy):
        return ((z + dz + 4) % 4) * 8 + ((x + dx + 4) % 4) * 2 + yy

    def nbr(p, axis_b, delta):
        return (g, at(delta, 0, y) if (p == 0) != axis_b else at(0, delta, y))

    def rdma(src, dst, ss, rs, dev):
        return pltpu.make_async_remote_copy(src_ref=src, dst_ref=dst, send_sem=ss, recv_sem=rs,
                                            device_id=dev, device_id_type=MESH)

    scope = [None]

    def phase(name):
        if scope[0] is not None:
            scope[0].__exit__(None, None, None)
            scope[0] = None
        if name:
            scope[0] = jax.named_scope(name)
            scope[0].__enter__()

    phase("enter")
    barrier = pltpu.get_barrier_semaphore()

    def greet(i, carry):
        pl.semaphore_signal(barrier, inc=1, device_id=(g, (c + i) % NPEER), device_id_type=MESH)
        return carry

    lax.fori_loop(1, NPEER, greet, 0)
    places = [(0, 0)] + [(d, 0) for d in range(1, 4)] + [(0, d) for d in range(1, 4)]
    for dg in range(1, 4):
        for dz, dx in places:
            for yy in range(2):
                pl.semaphore_signal(barrier, inc=1, device_id=((g + dg) % 4, at(dz, dx, yy)), device_id_type=MESH)

    own_copy = pltpu.make_async_copy(cache_ref, cbuf.at[0], csem.at[0])
    own_copy.start()
    vu_copy = pltpu.make_async_copy(vu_ref, vuv, csem.at[2])
    vu_copy.start()
    op_copy = pltpu.make_async_copy(op_ref, opv, csem.at[1])
    op_copy.start()
    for t in range(4):
        for s in range(4):
            qown[t, 4 * s:4 * s + 4] = q_ref[t, 0, s]
    for t in range(3):
        qbuf[0, t, 0, 0] = qown[t]

    lane = lanes_of((ROWS, 128))
    lane_k = lanes_of((ROWS, 4))
    row_s = lax.broadcasted_iota(jnp.int32, (ROWS, 4), 0) // 4
    for t in range(4):
        q = qown[t]
        logits = []
        for u in range(t + 1):
            lg = lax.dot_general(q, nl_ref[u, 0], (((1,), (1,)), ((), ())), preferred_element_type=F32)
            logits.append(jnp.where(lane_k == row_s, lg * SCALE2, LOW))
        top = jnp.max(logits[0], axis=1, keepdims=True)
        for lg in logits[1:]:
            top = jnp.maximum(top, jnp.max(lg, axis=1, keepdims=True))
        total = jnp.zeros((ROWS, 1), F32)
        acc = jnp.zeros((ROWS, LATENT), F32)
        for u in range(t + 1):
            w = jnp.where(lane_k == row_s, jnp.exp2(logits[u] - top), 0.0)
            total = total + jnp.sum(w, axis=1, keepdims=True)
            val = nl_ref[u, 0][:, :LATENT]
            whi = w.astype(BF)
            wlo = (w - whi.astype(F32)).astype(BF)
            acc = acc + (jnp.dot(whi, val, preferred_element_type=F32)
                         + jnp.dot(wlo, val, preferred_element_type=F32))
        fo[t] = acc
        fst[t, 0] = jnp.broadcast_to(top, (ROWS, 128))
        fst[t, 1] = jnp.broadcast_to(total, (ROWS, 128))

    pl.semaphore_wait(barrier, NPEER - 1 + 42)
    phase("prep")

    def hsems(p, t, d):
        n = (p * NPART + t) * 4 + d
        return hsend.at[n], hrecv.at[n]

    def h0(t, d):
        return rdma(qown.at[t], qbuf.at[0, t, 0, (4 - d) % 4], *hsems(0, t, d), (g, at(0, d, y)))

    def h1(t, d):
        return rdma(qown.at[t], qbuf.at[1, t, 0, (4 - d) % 4], *hsems(1, t, d), (g, at(d, 0, 1 - y)))

    def hs(hh, yy, d):
        p = g % 2
        t = 3 + g // 2
        dz = jnp.where(p == 0, 0, d)
        dev = (2 * hh + y, at(dz, d - dz, yy))
        n = (p * NPART + t) * 4 + d
        return rdma(qown.at[3], qbuf.at[p, t, 0, (4 - d) % 4],
                    hsend.at[40 + (2 * hh + yy) * 4 + d], hrecv.at[n], dev)

    def sems(p, t, i):
        n = (p * NPART + t) * 4 + i
        return gsend.at[n], grecv.at[n]

    def fwd_sign(p, t):
        return 1 if (t + p) % 2 == 0 else -1

    def g2(p, t, sign):
        return rdma(qbuf.at[p, t, 0], qbuf.at[p, t, 3 if sign > 0 else 1],
                    *sems(p, t, 0 if sign > 0 else 1), nbr(p, False, sign))

    def g2f(p, t, sign):
        half = pl.ds(0, 2) if sign > 0 else pl.ds(2, 2)
        return rdma(qbuf.at[p, t, 3 if sign > 0 else 1, half], qbuf.at[p, t, 2, half],
                    *sems(p, t, 2 if sign > 0 else 3), nbr(p, False, sign))

    def send2(p, t):
        if t < 3:
            for d in ((1, 2, 3) if p == 0 else (0, 1, 2, 3)):
                (h0 if p == 0 else h1)(t, d).wait_recv()
        else:
            s = (t - 3) * 2 + p
            mine = (g == s) & (y == k)
            for d in range(4):
                n = (p * NPART + t) * 4 + d
                cp = rdma(qown.at[3], qbuf.at[p, t, 0, (4 - d) % 4], hsend.at[0], hrecv.at[n], (g, c))
                if d == 0:
                    pl.when(jnp.logical_not(mine))(cp.wait_recv)
                else:
                    cp.wait_recv()
        g2(p, t, 1).start()
        g2(p, t, -1).start()

    def relay2(p, t):
        for sign in (1, -1):
            g2(p, t, sign).wait_recv()
            g2f(p, t, sign).start()

    def ready(p, t):
        for sign in (1, -1):
            g2f(p, t, sign).wait_recv()

    order = [(0, 0), (1, 0), (0, 1), (1, 1), (0, 3), (1, 3), (0, 4), (1, 4), (1, 2), (0, 2)]
    slot_u = [u for u in order if u[1] >= 3]

    for t in range(2):
        for d in (1, 3, 2):
            h0(t, d).start()
        for d in (0, 1, 3, 2):
            h1(t, d).start()
    targets = [(hh, yy, d) for d in (0, 1, 3, 2) for hh in range(2) for yy in range(2)]
    for hh, yy, d in targets:
        if d == 0:
            mine = (2 * hh + y == g) & (y == yy)
            pl.when(jnp.logical_not(mine))(hs(hh, yy, d).start)
        else:
            hs(hh, yy, d).start()

    @pl.when(y == k)
    def _():
        qbuf[g % 2, 3 + g // 2, 0, 0] = qown[3]

    for t in range(2, 3):
        for d in (1, 3, 2):
            h0(t, d).start()
        for d in (0, 1, 3, 2):
            h1(t, d).start()
    swap = rdma(cache_ref, cbuf.at[1], csem.at[3], csem.at[4], (g + 1 - 2 * k, c))
    swap.start()
    phase("g1")
    for u in order[:4]:
        send2(*u)
    phase("g2")
    relay2(*order[0])
    for u in order[4:6]:
        send2(*u)
    relay2(*order[1])
    for u in order[6:]:
        send2(*u)
    own_copy.wait()

    nj = 4
    wj = CTX // nj
    start_pos = c * CTX

    def attend(p, t):
        if t < 3:
            keys = cbuf.at[0]
            limit = len_ref[g] - start_pos
        else:
            d = don_ref[(t - 3) * 2 + p]
            keys = cbuf.at[jnp.where(d % 2 == k, 0, 1)]
            limit = jnp.where(d // 2 == h, len_ref[d] - start_pos, 0)
        q = qbuf[p, t].reshape(UNIT, KEYW)
        top = jnp.full((UNIT, 1), FLOOR, F32)
        for j in range(nj):
            pos = lax.broadcasted_iota(jnp.int32, (1, wj), 1) + j * wj
            bias = jnp.where(pos < limit, 0.0, LOW)
            sc = jnp.dot(q, keys[:, j * wj:(j + 1) * wj], preferred_element_type=F32) * SCALE2 + bias
            scr[:, j * wj:(j + 1) * wj] = sc
            top = jnp.maximum(top, jnp.max(sc, axis=1, keepdims=True))
        top = rounded(top)
        total = jnp.zeros((UNIT, 1), F32)
        acc = jnp.zeros((UNIT, LATENT), F32)
        for j in range(nj):
            w = jnp.exp2(scr[:, j * wj:(j + 1) * wj] - top)
            total = total + jnp.sum(w, axis=1, keepdims=True)
            acc = acc + lax.dot_general(w.astype(BF), keys[:LATENT, j * wj:(j + 1) * wj],
                                        (((1,), (1,)), ((), ())), preferred_element_type=F32)
        obuf[p, t] = acc.astype(BF).reshape(4, 4, ROWS, LATENT)
        hi = rounded(total)
        lo = total - hi
        for a in range(4):
            tile = jnp.zeros((ROWS, 128), F32)
            for b in range(4):
                rows = slice((a * 4 + b) * ROWS, (a * 4 + b + 1) * ROWS)
                tile = jnp.where(lane == b, top[rows], tile)
                tile = jnp.where(lane == 4 + b, hi[rows], tile)
                tile = jnp.where(lane == 8 + b, lo[rows], tile)
            stat[p, t, a] = tile.astype(BF)

    def rsem(p, t, i):
        n = (p * NPART + t) * 8 + i
        return rsend.at[n], rrecv.at[n]

    def a1(p, t, sign):
        i = 0 if sign > 0 else 1
        half = pl.ds(0, 2) if sign > 0 else pl.ds(2, 2)
        dev = nbr(p, False, sign)
        return (rdma(obuf.at[p, t, 2, half], ra.at[p, t, i], *rsem(p, t, i), dev),
                rdma(stat.at[p, t, 2], ras.at[p, t, i], *rsem(p, t, 2 + i), dev))

    def a2(p, t, sign):
        i = 0 if sign > 0 else 1
        a = 1 if sign > 0 else 3
        dev = nbr(p, False, sign)
        return (rdma(obuf.at[p, t, a], rc.at[p, t, i], *rsem(p, t, 4 + i), dev),
                rdma(stat.at[p, t, a], rcs.at[p, t, i], *rsem(p, t, 6 + i), dev))

    def back(p, t, d):
        if t < 3:
            dev = (g, at(0, d, y) if p == 0 else at(d, 0, 1 - y))
            i = t * 7 + (d - 1 if p == 0 else 3 + d)
            return (rdma(obuf.at[p, t, 0, d], rd.at[i], dsend.at[2 * i], drecv.at[2 * i], dev),
                    rdma(stat.at[p, t, 0], rds.at[i], dsend.at[2 * i + 1], drecv.at[2 * i + 1], dev))
        s = (t - 3) * 2 + p
        dev = (s, at(0, d, k) if p == 0 else at(d, 0, k))
        i = (2 * h + y) * 4 + d
        j = 2 * (s * 4 + d)
        return (rdma(obuf.at[p, t, 0, d], rf.at[i], fsend.at[j], frecv.at[2 * i], dev),
                rdma(stat.at[p, t, 0], rfs.at[i], fsend.at[j + 1], frecv.at[2 * i + 1], dev))

    def start(pair):
        for cp in pair:
            cp.start()

    def got(pair):
        for cp in pair:
            cp.wait_recv()

    def gone(pair):
        for cp in pair:
            cp.wait_send()

    def only(pair, keep):
        return jnp.where(keep, pair[0], 4 * FLOOR), jnp.where(keep, pair[1], 0.0)

    def shifted(pair, b):
        if b == 0:
            return pair
        return pltpu.roll(pair[0], 128 - b, 1), pltpu.roll(pair[1], 128 - b, 1)

    def begin(p, t):
        start(a1(p, t, 1))
        start(a1(p, t, -1))

    def r1(p, t):
        for i, sign in ((0, 1), (1, -1)):
            got(a1(p, t, sign))
            a = 1 if i == 0 else 3
            inside = (lane < 2) if i == 0 else (lane >= 2) & (lane < 4)
            top, total, (f0, f1) = combine([stats(stat[p, t, a]), only(stats(ras[p, t, i]), inside)])
            for b in range(2):
                bb = 2 * i + b
                o = (obuf[p, t, a, bb].astype(F32) * f0[:, bb:bb + 1]
                     + ra[p, t, i, b].astype(F32) * f1[:, bb:bb + 1])
                obuf[p, t, a, bb] = o.astype(BF)
            stat[p, t, a] = packed(top, total)
            start(a2(p, t, sign))

    def r2(p, t):
        got(a2(p, t, 1))
        got(a2(p, t, -1))
        top, total, (f0, f1, f2) = combine([stats(stat[p, t, 0]), stats(rcs[p, t, 0]), stats(rcs[p, t, 1])])
        for b in (2, 1, 3, 0):
            o = (obuf[p, t, 0, b].astype(F32) * f0[:, b:b + 1] + rc[p, t, 0, b].astype(F32) * f1[:, b:b + 1]
                 + rc[p, t, 1, b].astype(F32) * f2[:, b:b + 1])
            obuf[p, t, 0, b] = o.astype(BF)
        stat[p, t, 0] = packed(top, total)
        if t < 3:
            for d in ((2, 1, 3) if p == 0 else (2, 1, 3, 0)):
                start(back(p, t, d))
        else:
            s = (t - 3) * 2 + p
            mine = (g == s) & (y == k)
            for d in (2, 1, 3):
                start(back(p, t, d))

            @pl.when(jnp.logical_not(mine))
            def _():
                start(back(p, t, 0))

            @pl.when(mine)
            def _():
                rf[(2 * h + y) * 4] = obuf[p, t, 0, 0]
                rfs[(2 * h + y) * 4] = stat[p, t, 0]

    att = [None] * 4

    def finish(t, parts, outs):
        parts = parts + [(fst[t, 0], fst[t, 1])]
        _, total, fs = combine(parts)
        o = fo[t] * fs[-1][:, 0:1]
        for f, v in zip(fs[:-1], outs):
            o = o + v().astype(F32) * f[:, 0:1]
        att[t] = (o / total[:, 0:1]).astype(BF)

    def fin_step(t):
        parts = [stats(stat[0, t, 0])]
        outs = [lambda: obuf[0, t, 0, 0]]
        for p in range(2):
            for d in ((1, 2, 3) if p == 0 else (0, 1, 2, 3)):
                got(back(p, t, d))
                i = t * 7 + (d - 1 if p == 0 else 3 + d)
                parts.append(shifted(stats(rds[i]), d))
                outs.append(functools.partial(lambda i: rd[i], i))
        finish(t, parts, outs)

    def fin_slot():
        parts, outs = [], []
        for i in range(16):
            cps = (rdma(obuf.at[0, 3, 0, 0], rf.at[i], fsend.at[0], frecv.at[2 * i], (g, c)),
                   rdma(stat.at[0, 3, 0], rfs.at[i], fsend.at[1], frecv.at[2 * i + 1], (g, c)))
            if i % 4 == 0:
                mine = (y == k) & (i // 4 == 2 * h + y)
                pl.when(jnp.logical_not(mine))(functools.partial(got, cps))
            else:
                got(cps)
            parts.append(shifted(stats(rfs[i]), i % 4))
            outs.append(functools.partial(lambda i: rf[i], i))
        finish(3, parts, outs)

    n_units = len(order)
    relayed = order[:2]
    lag1, lag2 = 2, 4
    for i in range(n_units + lag2):
        phase("r%d" % i)
        if lag2 <= i:
            r2(*order[i - lag2])
        if lag1 <= i < n_units + lag1:
            r1(*order[i - lag1])
        if i < n_units:
            for u in order[:i + 3]:
                if u not in relayed:
                    relay2(*u)
                    relayed.append(u)
            phase("w%d" % i)
            ready(*order[i])
            if order[i] == slot_u[0]:
                swap.wait()
            phase("attend%d" % i)
            attend(*order[i])
            begin(*order[i])
        if i == n_units:
            phase("fin0")
            fin_step(0)
            fin_step(1)
    phase("fin")
    fin_slot()
    fin_step(2)

    phase("tail")
    attended = jnp.concatenate(att, axis=0)
    vu_copy.wait()
    op_copy.wait()
    row_head = lax.broadcasted_iota(jnp.int32, (64, 128), 0) % 4
    pieces = []
    for head in range(4):
        hv = jnp.dot(attended, vuv[head], preferred_element_type=F32)
        pieces.append(jnp.where(row_head == head, hv, 0.0).astype(BF))
    spread = jnp.concatenate(pieces, axis=1)
    pick = (lax.broadcasted_iota(jnp.int32, (ROWS, 64), 1) // 4
            == lax.broadcasted_iota(jnp.int32, (ROWS, 64), 0))
    joined = jnp.dot(jnp.where(pick, 1.0, 0.0).astype(BF), spread, preferred_element_type=F32).astype(BF)

    def outc(dest, rel):
        return rdma(sbuf.at[dest], rbuf.at[rel], xsend.at[dest], xrecv.at[rel], (g, dest))

    width = 8 * OUTW
    for blk in range(4):
        term = jnp.dot(joined, opv[:, blk * width:(blk + 1) * width], preferred_element_type=F32)
        for i in range(8):
            sbuf[blk * 8 + i, :, :OUTW] = term[:, i * OUTW:(i + 1) * OUTW].astype(BF)

    def send_out(i, carry):
        outc((c + i) % NPEER, (NPEER - i) % NPEER).start()
        return carry

    lax.fori_loop(1, NPEER, send_out, 0)
    phase("outx")

    for hh, yy, d in targets:
        if d == 0:
            mine = (2 * hh + y == g) & (y == yy)
            pl.when(jnp.logical_not(mine))(hs(hh, yy, d).wait_send)
        else:
            hs(hh, yy, d).wait_send()
    for p, t in order:
        if t < 3:
            for d in ((1, 2, 3) if p == 0 else (0, 1, 2, 3)):
                (h0 if p == 0 else h1)(t, d).wait_send()
                gone(back(p, t, d))
        else:
            for d in (1, 2, 3):
                gone(back(p, t, d))
            mine = (g == (t - 3) * 2 + p) & (y == k)
            pl.when(jnp.logical_not(mine))(functools.partial(gone, back(p, t, 0)))
        for sign in (1, -1):
            g2(p, t, sign).wait_send()
            g2f(p, t, sign).wait_send()
            gone(a1(p, t, sign))
            gone(a2(p, t, sign))

    res = sbuf[c][:, :OUTW].astype(F32)
    for rel in range(1, NPEER):
        pltpu.make_async_remote_copy(src_ref=sbuf.at[0], dst_ref=rbuf.at[rel], send_sem=xsend.at[0],
                                     recv_sem=xrecv.at[rel], device_id=(g, c), device_id_type=MESH).wait_recv()
        res = res + rbuf[rel][:, :OUTW].astype(F32)
    for t in range(4):
        out_ref[t, 0] = res[4 * t:4 * t + 4].astype(BF)

    def sent_out(i, carry):
        outc((c + i) % NPEER, (NPEER - i) % NPEER).wait_send()
        return carry

    lax.fori_loop(1, NPEER, sent_out, 0)
    phase(None)


def body(cache, queries, new_latent, lengths, donor, value_up, out_proj):
    keys = jnp.swapaxes(cache[0], 0, 1)
    VM, SM, ANY = pltpu.VMEM, pltpu.SMEM, pl.ANY
    U = (2, NPART)
    dma = pltpu.SemaphoreType.DMA
    return pl.pallas_call(
        kernel,
        out_shape=jax.ShapeDtypeStruct((4, 1, 4, OUTW), BF),
        in_specs=[pl.BlockSpec(memory_space=m) for m in (SM, SM, VM, VM, ANY, ANY, ANY)],
        out_specs=pl.BlockSpec(memory_space=VM),
        scratch_shapes=[
            VM((2, KEYW, CTX), BF),
            VM((4, ROWS, KEYW), BF),
            VM(U + (4, 4, ROWS, KEYW), BF),
            VM(U + (4, 4, ROWS, LATENT), BF),
            VM(U + (4, ROWS, 128), BF),
            VM(U + (2, 2, ROWS, LATENT), BF), VM(U + (2, ROWS, 128), BF),
            VM(U + (2, 4, ROWS, LATENT), BF), VM(U + (2, ROWS, 128), BF),
            VM((21, ROWS, LATENT), BF), VM((21, ROWS, 128), BF),
            VM((16, ROWS, LATENT), BF), VM((16, ROWS, 128), BF),
            VM((NPEER, ROWS, 256), BF), VM((NPEER, ROWS, 256), BF),
            VM((512, 7168), BF), VM((4, LATENT, 128), BF),
            VM((UNIT, CTX), F32),
            VM((4, ROWS, LATENT), F32), VM((4, 2, ROWS, 128), F32),
            dma((5,)), dma((56,)), dma((40,)), dma((40,)), dma((40,)), dma((80,)), dma((80,)),
            dma((NPEER,)), dma((NPEER,)), dma((42,)), dma((42,)), dma((32,)), dma((32,)),
        ],
        compiler_params=pltpu.CompilerParams(collective_id=0, has_side_effects=True,
                                             vmem_limit_bytes=56 * 1024 * 1024),
        name="mla_step",
    )(lengths, donor, queries, new_latent, keys, value_up, out_proj)


def solution(mesh):
    return jax.shard_map(
        body,
        mesh=mesh,
        in_specs=(
            P("grp", "ctx", None),
            P(None, "grp", None, "ctx", None),
            P(None, "grp", None, None),
            P(),
            P(),
            P("ctx", None, None),
            P("ctx", None),
        ),
        out_specs=P(None, "grp", None, "ctx"),
        check_vma=False,
    )
```

time: 128 us -> 79.3 us (0.62)
  Pallas kernels: 117 us -> 77.8 us
  other arithmetic: 4.06 us -> 0 us
  local copies, waits for them, and re-layouts: 4.79 us -> 1.3 us
    pallas_call x1, Pallas kernels: 117 us -> 77.8 us  [body(): pl.pallas_call(kernel, out_shape=jax.ShapeDtypeStruct((4, 1, 4, OUTW), BF...]
    reshape x3 -> x0, local copies, waits for them, and re-layouts: 4.21 us -> none  [the longest x1 1.55 us: body(): q = queries.reshape(4, ROWS, KEYW)]
    reduce_sum x2 -> x0, other arithmetic: 2.14 us -> none  [the longest x1 1.29 us: body(): jnp.sum(jnp.where(jnp.arange(4, dtype=jnp.int32) == g, lengths, 0)) - start]
    unnamed x0 -> x1, local copies, waits for them, and re-layouts: none -> 1.3 us
where the time goes in v2:
time: 79.3 us; the launch traced here: 79.1 us
  Pallas kernels  77.8 us (98%)
  local copies, waits for them, and re-layouts  1.3 us (2%)
    pallas_call x1, Pallas kernels, body(): pl.pallas_call(kernel, out_shape=jax.ShapeDtypeStruct((4, 1, 4, OUTW), BF...  77.8 us

profile of v2, /device:TPU:0, one launch (start us, length us, event | category | flops | bytes accessed | tf_op | source)
XLA Modules:
  0.0 79.1 jit_solution(13750820763364987954)
XLA Ops:
  0.0 77.8 %mla_step.1 = bf16[4,1,4,224]{3,2,1,0:T(4,128)(2,1)} custom-call(s32[4]{0:T(128)} %len_ref.1, s32[4]{0:T(128)} %don_ref.1, bf16[4,1,4,4,576]{4,3,2,1,0:T(4,128)(2,1)} %q_ref.1, bf16[4,1,4,576]{3,2,1,0:T(4,128)(2,1)} %nl_ref.1, bf16[576,2048]{1,0:T(8,128)(2,1)} %bitcast.3, bf16[4,512,128]{2,1,0:T(8,128)(2,1)} %vu_ref.1, bf16[512,7168]{1,0:T(8,128)(2,1)} %op_ref.1), custom_call_target="tpu_custom_call" | custom-call | tf_op jit(solution)/shard_map/mla_step/pallas_call | solution.py:518
  77.8 1.3 %copy.9 = bf16[4,1,4,224]{3,2,1,0:T(4,128)(2,1)} copy(bf16[4,1,4,224]{3,2,1,0:T(4,128)(2,1)} %mla_step.1) | data formatting | bytes 14336

commit v3 on v2

v3 whole, which is shorter than its diff:
```python
import functools

import jax
import jax.numpy as jnp
from jax import lax
from jax.experimental import pallas as pl
from jax.experimental.pallas import tpu as pltpu
from jax.sharding import PartitionSpec as P

MESH = pl.DeviceIdType.MESH
LATENT = 512
KEYW = 576
CTX = 2048
ROWS = 16
UNIT = 256
NPART = 5
OUTW = 224
NPEER = 32
SCALE2 = (192.0 ** -0.5) * 1.4426950408889634
LOW = -1e30
FLOOR = -1e29
BF = jnp.bfloat16
F32 = jnp.float32


def rounded(v):
    return v.astype(BF).astype(F32)


def lanes_of(shape):
    return lax.broadcasted_iota(jnp.int32, shape, 1)


def stats(tile):
    t = tile.astype(F32)
    return t, pltpu.roll(t, 124, 1) + pltpu.roll(t, 120, 1)


def combine(parts):
    top = parts[0][0]
    for t, _ in parts[1:]:
        top = jnp.maximum(top, t)
    factors = [jnp.exp2(t - top) for t, _ in parts]
    total = factors[0] * parts[0][1]
    for f, (_, v) in zip(factors[1:], parts[1:]):
        total = total + f * v
    return top, total, factors


def packed(top, total):
    lane = lanes_of(top.shape)
    hi = rounded(total)
    lo = total - hi
    return jnp.where(lane < 4, top, jnp.where(lane < 8, pltpu.roll(hi, 4, 1), pltpu.roll(lo, 8, 1))).astype(BF)


def kernel(len_ref, don_ref, q_ref, nl_ref, cache_ref, vu_ref, op_ref, out_ref,
           cbuf, qown, qbuf, obuf, stat, ra, ras, rc, rcs, rd, rds, rf, rfs,
           sbuf, rbuf, opv, vuv, fo, fst,
           csem, hsend, hrecv, gsend, grecv, rsend, rrecv, xsend, xrecv, dsend, drecv, fsend, frecv):
    g = lax.axis_index("grp")
    c = lax.axis_index("ctx")
    h = g // 2
    k = g % 2
    z = c // 8
    x = (c // 2) % 4
    y = c % 2
    other = c + 1 - 2 * y

    def at(dz, dx, yy):
        return ((z + dz + 4) % 4) * 8 + ((x + dx + 4) % 4) * 2 + yy

    def line(p, t, d):
        return (0, d) if (p + t) % 2 == 0 else (d, 0)

    def nbr(p, t, d):
        dx, dz = line(p, t, d)
        return (g, at(dz, dx, y))

    def rdma(src, dst, ss, rs, dev):
        return pltpu.make_async_remote_copy(src_ref=src, dst_ref=dst, send_sem=ss, recv_sem=rs,
                                            device_id=dev, device_id_type=MESH)

    scope = [None]

    def phase(name):
        if scope[0] is not None:
            scope[0].__exit__(None, None, None)
            scope[0] = None
        if name:
            scope[0] = jax.named_scope(name)
            scope[0].__enter__()

    phase("enter")
    barrier = pltpu.get_barrier_semaphore()

    def greet(i, carry):
        pl.semaphore_signal(barrier, inc=1, device_id=(g, (c + i) % NPEER), device_id_type=MESH)
        return carry

    lax.fori_loop(1, NPEER, greet, 0)
    places = [(0, 0)] + [(d, 0) for d in range(1, 4)] + [(0, d) for d in range(1, 4)]
    for dg in range(1, 4):
        for dz, dx in places:
            for yy in range(2):
                pl.semaphore_signal(barrier, inc=1, device_id=((g + dg) % 4, at(dz, dx, yy)), device_id_type=MESH)

    own_copy = pltpu.make_async_copy(cache_ref, cbuf.at[0], csem.at[0])
    own_copy.start()
    vu_copy = pltpu.make_async_copy(vu_ref, vuv, csem.at[2])
    vu_copy.start()
    op_copy = pltpu.make_async_copy(op_ref, opv, csem.at[1])
    op_copy.start()
    for t in range(4):
        for s in range(4):
            qown[t, 4 * s:4 * s + 4] = q_ref[t, 0, s]
    for t in range(3):
        qbuf[0, t, 0, 0] = qown[t]

    lane = lanes_of((ROWS, 128))
    lane_k = lanes_of((ROWS, 4))
    row_s = lax.broadcasted_iota(jnp.int32, (ROWS, 4), 0) // 4
    for t in range(4):
        q = qown[t]
        logits = []
        for u in range(t + 1):
            lg = lax.dot_general(q, nl_ref[u, 0], (((1,), (1,)), ((), ())), preferred_element_type=F32)
            logits.append(jnp.where(lane_k == row_s, lg * SCALE2, LOW))
        top = jnp.max(logits[0], axis=1, keepdims=True)
        for lg in logits[1:]:
            top = jnp.maximum(top, jnp.max(lg, axis=1, keepdims=True))
        total = jnp.zeros((ROWS, 1), F32)
        acc = jnp.zeros((ROWS, LATENT), F32)
        for u in range(t + 1):
            w = jnp.where(lane_k == row_s, jnp.exp2(logits[u] - top), 0.0)
            total = total + jnp.sum(w, axis=1, keepdims=True)
            val = nl_ref[u, 0][:, :LATENT]
            whi = w.astype(BF)
            wlo = (w - whi.astype(F32)).astype(BF)
            acc = acc + (jnp.dot(whi, val, preferred_element_type=F32)
                         + jnp.dot(wlo, val, preferred_element_type=F32))
        fo[t] = acc
        fst[t, 0] = jnp.broadcast_to(top, (ROWS, 128))
        fst[t, 1] = jnp.broadcast_to(total, (ROWS, 128))

    pl.semaphore_wait(barrier, NPEER - 1 + 42)
    phase("prep")

    def hsems(p, t, d):
        n = (p * NPART + t) * 4 + d
        return hsend.at[n], hrecv.at[n]

    def along(p, t, d):
        dz, dx = line(p, t, d)
        return rdma(qbuf.at[p, t, 0, 0], qbuf.at[p, t, 0, (4 - d) % 4], *hsems(p, t, d), (g, at(dz, dx, y)))

    def across(t):
        return rdma(qown.at[t], qbuf.at[1, t, 0, 0], *hsems(1, t, 0), (g, other))

    def handed(hh, yy):
        n = ((g % 2) * NPART + 3 + g // 2) * 4
        return rdma(qown.at[3], qbuf.at[g % 2, 3 + g // 2, 0, 0],
                    hsend.at[40 + 2 * hh + yy], hrecv.at[n], (2 * hh + y, at(0, 0, yy)))

    def handed_in(p, t):
        n = (p * NPART + t) * 4
        return rdma(qown.at[3], qbuf.at[p, t, 0, 0], hsend.at[0], hrecv.at[n], (g, c))

    def sems(p, t, i):
        n = (p * NPART + t) * 4 + i
        return gsend.at[n], grecv.at[n]

    def g2(p, t, sign):
        return rdma(qbuf.at[p, t, 0], qbuf.at[p, t, 3 if sign > 0 else 1],
                    *sems(p, t, 0 if sign > 0 else 1), nbr(p, t, sign))

    def g2f(p, t, sign):
        half = pl.ds(0, 2) if sign > 0 else pl.ds(2, 2)
        return rdma(qbuf.at[p, t, 3 if sign > 0 else 1, half], qbuf.at[p, t, 2, half],
                    *sems(p, t, 2 if sign > 0 else 3), nbr(p, t, sign))

    def send1(p, t):
        for d in (1, 3, 2):
            along(p, t, d).start()

    def send2(p, t):
        for d in range(1, 4):
            along(p, t, d).wait_recv()
        g2(p, t, 1).start()
        g2(p, t, -1).start()

    def spread(p, t):
        if t < 3:
            across(t).wait_recv()
        else:
            mine = (g == (t - 3) * 2 + p) & (y == k)
            pl.when(jnp.logical_not(mine))(handed_in(p, t).wait_recv)
        send1(p, t)

    def relay2(p, t):
        for sign in (1, -1):
            g2(p, t, sign).wait_recv()
            g2f(p, t, sign).start()

    def ready(p, t):
        for sign in (1, -1):
            g2f(p, t, sign).wait_recv()

    early = [(0, 0), (0, 1)]
    middle = [(1, 0), (1, 1)]
    late = [(1, 2), (0, 2)]
    slot_u = [(0, 3), (1, 3), (0, 4), (1, 4)]
    order = early + middle + slot_u + late

    def handed_do(what):
        for hh in range(2):
            for yy in range(2):
                mine = (2 * hh + y == g) & (y == yy)
                cp = handed(hh, yy)
                pl.when(jnp.logical_not(mine))(cp.start if what else cp.wait_send)

    across(0).start()
    across(1).start()
    send1(0, 0)
    send1(0, 1)
    across(2).start()
    handed_do(True)
    send1(0, 2)

    @pl.when(y == k)
    def _():
        qbuf[g % 2, 3 + g // 2, 0, 0] = qown[3]

    swap = rdma(cache_ref, cbuf.at[1], csem.at[3], csem.at[4], (g + 1 - 2 * k, c))

    nj = 2
    wj = CTX // nj
    start_pos = c * CTX

    def attend(groups):
        n = len(groups)
        p, t, _ = groups[0]
        if t < 3:
            keys = cbuf.at[0]
            limit = len_ref[g] - start_pos
        else:
            d = don_ref[(t - 3) * 2 + p]
            keys = cbuf.at[jnp.where(d % 2 == k, 0, 1)]
            limit = jnp.where(d // 2 == h, len_ref[d] - start_pos, 0)
        q = jnp.concatenate([qbuf[p, t, a].reshape(64, KEYW) for p, t, a in groups], axis=0)

        def score(j):
            pos = lax.broadcasted_iota(jnp.int32, (1, wj), 1) + j * wj
            bias = jnp.where(pos < limit, 0.0, LOW)
            return jnp.dot(q, keys[:, j * wj:(j + 1) * wj], preferred_element_type=F32) * SCALE2 + bias

        top = total = acc = None
        later = score(0)
        for j in range(nj):
            sc = later
            if j + 1 < nj:
                later = score(j + 1)
            peak = rounded(jnp.maximum(jnp.max(sc, axis=1, keepdims=True), FLOOR if top is None else top))
            w = jnp.exp2(sc - peak)
            part = jnp.sum(w, axis=1, keepdims=True)
            val = lax.dot_general(w.astype(BF), keys[:LATENT, j * wj:(j + 1) * wj],
                                  (((1,), (1,)), ((), ())), preferred_element_type=F32)
            if top is None:
                total, acc = part, val
            else:
                scale = jnp.exp2(top - peak)
                total = total * scale + part
                acc = acc * scale + val
            top = peak
        hi = rounded(total)
        lo = total - hi
        for i, (p, t, a) in enumerate(groups):
            obuf[p, t, a] = acc[64 * i:64 * i + 64].astype(BF).reshape(4, ROWS, LATENT)
            tile = jnp.zeros((ROWS, 128), F32)
            for b in range(4):
                part = slice((i * 4 + b) * ROWS, (i * 4 + b + 1) * ROWS)
                tile = jnp.where(lane == b, top[part], tile)
                tile = jnp.where(lane == 4 + b, hi[part], tile)
                tile = jnp.where(lane == 8 + b, lo[part], tile)
            stat[p, t, a] = tile.astype(BF)

    def rsem(p, t, i):
        n = (p * NPART + t) * 8 + i
        return rsend.at[n], rrecv.at[n]

    def a1(p, t, sign):
        i = 0 if sign > 0 else 1
        half = pl.ds(0, 2) if sign > 0 else pl.ds(2, 2)
        dev = nbr(p, t, sign)
        return (rdma(obuf.at[p, t, 2, half], ra.at[p, t, i], *rsem(p, t, i), dev),
                rdma(stat.at[p, t, 2], ras.at[p, t, i], *rsem(p, t, 2 + i), dev))

    def a2(p, t, sign):
        i = 0 if sign > 0 else 1
        a = 1 if sign > 0 else 3
        dev = nbr(p, t, sign)
        return (rdma(obuf.at[p, t, a], rc.at[p, t, i], *rsem(p, t, 4 + i), dev),
                rdma(stat.at[p, t, a], rcs.at[p, t, i], *rsem(p, t, 6 + i), dev))

    def back(p, t, d):
        dz, dx = line(p, t, d)
        if t < 3:
            dev = (g, at(dz, dx, y if p == 0 else 1 - y))
            i = t * 7 + (d - 1 if p == 0 else 3 + d)
            return (rdma(obuf.at[p, t, 0, d], rd.at[i], dsend.at[2 * i], drecv.at[2 * i], dev),
                    rdma(stat.at[p, t, 0], rds.at[i], dsend.at[2 * i + 1], drecv.at[2 * i + 1], dev))
        s = (t - 3) * 2 + p
        dev = (s, at(dz, dx, k))
        i = (2 * h + y) * 4 + d
        j = 2 * (s * 4 + d)
        return (rdma(obuf.at[p, t, 0, d], rf.at[i], fsend.at[j], frecv.at[2 * i], dev),
                rdma(stat.at[p, t, 0], rfs.at[i], fsend.at[j + 1], frecv.at[2 * i + 1], dev))

    def start(pair):
        for cp in pair:
            cp.start()

    def got(pair):
        for cp in pair:
            cp.wait_recv()

    def gone(pair):
        for cp in pair:
            cp.wait_send()

    def only(pair, keep):
        return jnp.where(keep, pair[0], 4 * FLOOR), jnp.where(keep, pair[1], 0.0)

    def shifted(pair, b):
        if b == 0:
            return pair
        return pltpu.roll(pair[0], 128 - b, 1), pltpu.roll(pair[1], 128 - b, 1)

    def begin(p, t):
        start(a1(p, t, 1))
        start(a1(p, t, -1))

    def r1(units):
        for p, t in units:
            got(a1(p, t, 1))
            got(a1(p, t, -1))
        for p, t in units:
            for i in range(2):
                a = 1 if i == 0 else 3
                inside = (lane < 2) if i == 0 else (lane >= 2) & (lane < 4)
                top, total, (f0, f1) = combine([stats(stat[p, t, a]), only(stats(ras[p, t, i]), inside)])
                for b in range(2):
                    bb = 2 * i + b
                    o = (obuf[p, t, a, bb].astype(F32) * f0[:, bb:bb + 1]
                         + ra[p, t, i, b].astype(F32) * f1[:, bb:bb + 1])
                    obuf[p, t, a, bb] = o.astype(BF)
                stat[p, t, a] = packed(top, total)
        for p, t in units:
            start(a2(p, t, 1))
            start(a2(p, t, -1))

    def r2(units):
        for p, t in units:
            got(a2(p, t, 1))
            got(a2(p, t, -1))
        for p, t in units:
            top, total, (f0, f1, f2) = combine([stats(stat[p, t, 0]), stats(rcs[p, t, 0]), stats(rcs[p, t, 1])])
            for b in range(4):
                o = (obuf[p, t, 0, b].astype(F32) * f0[:, b:b + 1] + rc[p, t, 0, b].astype(F32) * f1[:, b:b + 1]
                     + rc[p, t, 1, b].astype(F32) * f2[:, b:b + 1])
                obuf[p, t, 0, b] = o.astype(BF)
            stat[p, t, 0] = packed(top, total)
        for p, t in units:
            for d in (2, 1, 3):
                start(back(p, t, d))
            if t < 3:
                if p == 1:
                    start(back(p, t, 0))
            else:
                mine = (g == (t - 3) * 2 + p) & (y == k)

                @pl.when(jnp.logical_not(mine))
                def _():
                    start(back(p, t, 0))

                @pl.when(mine)
                def _():
                    rf[(2 * h + y) * 4] = obuf[p, t, 0, 0]
                    rfs[(2 * h + y) * 4] = stat[p, t, 0]

    att = [None] * 4

    def fold_in(t, parts, outs, last):
        parts = parts + [(fst[t, 0], fst[t, 1])]
        top, total, fs = combine(parts)
        o = fo[t] * fs[-1][:, 0:1]
        for f, v in zip(fs[:-1], outs):
            o = o + v.astype(F32) * f[:, 0:1]
        if last:
            att[t] = (o / total[:, 0:1]).astype(BF)
        else:
            fo[t] = o
            fst[t, 0] = top
            fst[t, 1] = total

    def fin_half(p, t):
        ds = (1, 2, 3) if p == 0 else (0, 1, 2, 3)
        for d in ds:
            got(back(p, t, d))
        where = [t * 7 + (d - 1 if p == 0 else 3 + d) for d in ds]
        parts = [shifted(stats(rds[i]), d) for i, d in zip(where, ds)]
        outs = [rd[i] for i in where]
        if p == 0:
            parts.append(stats(stat[0, t, 0]))
            outs.append(obuf[0, t, 0, 0])
        fold_in(t, parts, outs, p == 1)

    def fin_slot():
        for i in range(16):
            cps = (rdma(obuf.at[0, 3, 0, 0], rf.at[i], fsend.at[0], frecv.at[2 * i], (g, c)),
                   rdma(stat.at[0, 3, 0], rfs.at[i], fsend.at[1], frecv.at[2 * i + 1], (g, c)))
            if i % 4 == 0:
                mine = (y == k) & (i // 4 == 2 * h + y)
                pl.when(jnp.logical_not(mine))(functools.partial(got, cps))
            else:
                got(cps)
        fold_in(3, [shifted(stats(rfs[i]), i % 4) for i in range(16)], [rf[i] for i in range(16)], True)

    def each(f, units):
        for u in units:
            f(*u)

    def of(units, *dists):
        return [(p, t, a) for a in dists for p, t in units]

    phase("g1")
    each(spread, middle)
    each(send2, early)
    spread(*late[0])
    each(spread, slot_u)
    own_copy.wait()
    phase("B1")
    attend(of(early, 0))
    phase("g2")
    each(send2, middle)
    each(relay2, early)
    each(send2, late)
    swap.start()
    phase("B2")
    attend(of(early, 1, 3))
    phase("g3")
    each(send2, slot_u[:2])
    each(relay2, middle)
    each(send2, slot_u[2:])
    each(ready, early)
    phase("B3")
    attend(of(early, 2) + of(middle, 0))
    each(begin, early)
    phase("g4")
    each(relay2, late)
    phase("B4")
    attend(of(middle, 1, 3))
    phase("g5")
    each(relay2, slot_u[:2])
    each(ready, middle)
    each(ready, late)
    phase("B5")
    attend(of(middle, 2) + of(late, 2))
    each(begin, middle)
    each(begin, late)
    phase("g6")
    each(relay2, slot_u[2:])
    r1(early)
    swap.wait()

    def slot(i):
        phase("ws%d" % i)
        ready(*slot_u[i])
        phase("S%d" % i)
        attend(of(slot_u[i:i + 1], 0, 1, 2, 3))
        begin(*slot_u[i])
        phase("rs%d" % i)

    slot(0)
    slot(1)
    r1(middle)
    r2(early)
    slot(2)
    r1(slot_u[0:1])
    slot(3)
    r1(slot_u[1:2])
    r2(middle)
    phase("M3")
    attend(of(late, 1, 3) + of(late[:1], 0))
    phase("rm3")
    r1(late)
    r1(slot_u[2:3])
    r2(slot_u[0:1])
    fin_half(0, 0)
    fin_half(0, 1)
    phase("E")
    attend(of(late[1:], 0))
    phase("re")
    r1(slot_u[3:])
    r2(slot_u[1:2])
    fin_half(1, 0)
    fin_half(1, 1)
    phase("rlate")
    r2(late)
    phase("rs12")
    r2(slot_u[2:3])
    phase("rs13")
    r2(slot_u[3:])
    phase("f2")
    fin_half(0, 2)
    fin_half(1, 2)
    phase("fs")
    fin_slot()

    phase("tail")
    attended = jnp.concatenate(att, axis=0)
    vu_copy.wait()
    op_copy.wait()
    row_head = lax.broadcasted_iota(jnp.int32, (64, 128), 0) % 4
    pieces = []
    for head in range(4):
        hv = jnp.dot(attended, vuv[head], preferred_element_type=F32)
        pieces.append(jnp.where(row_head == head, hv, 0.0).astype(BF))
    spread = jnp.concatenate(pieces, axis=1)
    pick = (lax.broadcasted_iota(jnp.int32, (ROWS, 64), 1) // 4
            == lax.broadcasted_iota(jnp.int32, (ROWS, 64), 0))
    joined = jnp.dot(jnp.where(pick, 1.0, 0.0).astype(BF), spread, preferred_element_type=F32).astype(BF)

    def outc(dest, rel):
        return rdma(sbuf.at[dest], rbuf.at[rel], xsend.at[dest], xrecv.at[rel], (g, dest))

    width = 8 * OUTW
    for blk in range(4):
        term = jnp.dot(joined, opv[:, blk * width:(blk + 1) * width], preferred_element_type=F32)
        for i in range(8):
            dest = blk * 8 + i
            sbuf[dest, :, :OUTW] = term[:, i * OUTW:(i + 1) * OUTW].astype(BF)
        for i in range(8):
            dest = blk * 8 + i
            pl.when(dest != c)(outc(dest, (c - dest + NPEER) % NPEER).start)
    phase("outx")

    handed_do(False)
    for p, t in order:
        for d in (1, 2, 3):
            along(p, t, d).wait_send()
            gone(back(p, t, d))
        if t >= 3:
            mine = (g == (t - 3) * 2 + p) & (y == k)
            pl.when(jnp.logical_not(mine))(functools.partial(gone, back(p, t, 0)))
        elif p == 1:
            across(t).wait_send()
            gone(back(p, t, 0))
        for sign in (1, -1):
            g2(p, t, sign).wait_send()
            g2f(p, t, sign).wait_send()
            gone(a1(p, t, sign))
            gone(a2(p, t, sign))

    res = sbuf[c][:, :OUTW].astype(F32)
    for rel in range(1, NPEER):
        pltpu.make_async_remote_copy(src_ref=sbuf.at[0], dst_ref=rbuf.at[rel], send_sem=xsend.at[0],
                                     recv_sem=xrecv.at[rel], device_id=(g, c), device_id_type=MESH).wait_recv()
        res = res + rbuf[rel][:, :OUTW].astype(F32)
    for t in range(4):
        out_ref[t, 0] = res[4 * t:4 * t + 4].astype(BF)

    def sent_out(i, carry):
        outc((c + i) % NPEER, (NPEER - i) % NPEER).wait_send()
        return carry

    lax.fori_loop(1, NPEER, sent_out, 0)
    phase(None)


def body(cache, queries, new_latent, lengths, donor, value_up, out_proj):
    keys = jnp.swapaxes(cache[0], 0, 1)
    VM, SM, ANY = pltpu.VMEM, pltpu.SMEM, pl.ANY
    U = (2, NPART)
    dma = pltpu.SemaphoreType.DMA
    return pl.pallas_call(
        kernel,
        out_shape=jax.ShapeDtypeStruct((4, 1, 4, OUTW), BF),
        in_specs=[pl.BlockSpec(memory_space=m) for m in (SM, SM, VM, VM, ANY, ANY, ANY)],
        out_specs=pl.BlockSpec(memory_space=VM),
        scratch_shapes=[
            VM((2, KEYW, CTX), BF),
            VM((4, ROWS, KEYW), BF),
            VM(U + (4, 4, ROWS, KEYW), BF),
            VM(U + (4, 4, ROWS, LATENT), BF),
            VM(U + (4, ROWS, 128), BF),
            VM(U + (2, 2, ROWS, LATENT), BF), VM(U + (2, ROWS, 128), BF),
            VM(U + (2, 4, ROWS, LATENT), BF), VM(U + (2, ROWS, 128), BF),
            VM((21, ROWS, LATENT), BF), VM((21, ROWS, 128), BF),
            VM((16, ROWS, LATENT), BF), VM((16, ROWS, 128), BF),
            VM((NPEER, ROWS, 256), BF), VM((NPEER, ROWS, 256), BF),
            VM((512, 7168), BF), VM((4, LATENT, 128), BF),
            VM((4, ROWS, LATENT), F32), VM((4, 2, ROWS, 128), F32),
            dma((5,)), dma((44,)), dma((40,)), dma((40,)), dma((40,)), dma((80,)), dma((80,)),
            dma((NPEER,)), dma((NPEER,)), dma((42,)), dma((42,)), dma((32,)), dma((32,)),
        ],
        compiler_params=pltpu.CompilerParams(collective_id=0, has_side_effects=True,
                                             vmem_limit_bytes=56 * 1024 * 1024),
        name="mla_step",
    )(lengths, donor, queries, new_latent, keys, value_up, out_proj)


def solution(mesh):
    return jax.shard_map(
        body,
        mesh=mesh,
        in_specs=(
            P("grp", "ctx", None),
            P(None, "grp", None, "ctx", None),
            P(None, "grp", None, None),
            P(),
            P(),
            P("ctx", None, None),
            P("ctx", None),
        ),
        out_specs=P(None, "grp", None, "ctx"),
        check_vma=False,
    )
```

time: 79.3 us -> 69.7 us (0.88); the launches traced: 79.1 us -> 68.7 us
  Pallas kernels: 77.8 us -> 67.3 us
    pallas_call x1, Pallas kernels: 77.8 us -> 67.3 us  [body(): pl.pallas_call(kernel, out_shape=jax.ShapeDtypeStruct((4, 1, 4, OUTW), BF...]
where the time goes in v3:
time: 69.7 us; the launch traced here: 68.7 us
  Pallas kernels  67.3 us (97%)
  local copies, waits for them, and re-layouts  1.3 us (2%)
    pallas_call x1, Pallas kernels, body(): pl.pallas_call(kernel, out_shape=jax.ShapeDtypeStruct((4, 1, 4, OUTW), BF...  67.3 us

profile of v3, /device:TPU:0, one launch (start us, length us, event | category | flops | bytes accessed | tf_op | source)
XLA Modules:
  0.0 68.7 jit_solution(13565911245793110120)
XLA Ops:
  0.0 67.3 %mla_step.1 = bf16[4,1,4,224]{3,2,1,0:T(4,128)(2,1)} custom-call(s32[4]{0:T(128)} %len_ref.1, s32[4]{0:T(128)} %don_ref.1, bf16[4,1,4,4,576]{4,3,2,1,0:T(4,128)(2,1)} %q_ref.1, bf16[4,1,4,576]{3,2,1,0:T(4,128)(2,1)} %nl_ref.1, bf16[576,2048]{1,0:T(8,128)(2,1)} %bitcast.3, bf16[4,512,128]{2,1,0:T(8,128)(2,1)} %vu_ref.1, bf16[512,7168]{1,0:T(8,128)(2,1)} %op_ref.1), custom_call_target="tpu_custom_call" | custom-call | tf_op jit(solution)/shard_map/mla_step/pallas_call | solution.py:586
  67.4 1.3 %copy.9 = bf16[4,1,4,224]{3,2,1,0:T(4,128)(2,1)} copy(bf16[4,1,4,224]{3,2,1,0:T(4,128)(2,1)} %mla_step.1) | data formatting | bytes 14336

commit v4 on v3

--- a/solution.py
+++ b/solution.py
@@ -21,6 +21,7 @@
 FLOOR = -1e29
 BF = jnp.bfloat16
 F32 = jnp.float32
+XLINE = ((0, 0), (1, 0), (0, 2), (1, 3), (0, 4))
 
 
 def rounded(v):
@@ -34,6 +35,14 @@
 def stats(tile):
     t = tile.astype(F32)
     return t, pltpu.roll(t, 124, 1) + pltpu.roll(t, 120, 1)
+
+
+TILE = (0, 4, 9, 13)
+STAT = 8
+
+
+def chunk(tiles):
+    return jnp.concatenate(tiles, axis=1).astype(F32)
 
 
 def combine(parts):
@@ -55,8 +64,7 @@
 
 
 def kernel(len_ref, don_ref, q_ref, nl_ref, cache_ref, vu_ref, op_ref, out_ref,
-           cbuf, qown, qbuf, obuf, stat, ra, ras, rc, rcs, rd, rds, rf, rfs,
-           sbuf, rbuf, opv, vuv, fo, fst,
+           cbuf, qown, qbuf, obuf, ra, rc, bb, by, rd, rf, sbuf, rbuf, opv, vuv, fo, fst,
            csem, hsend, hrecv, gsend, grecv, rsend, rrecv, xsend, xrecv, dsend, drecv, fsend, frecv):
     g = lax.axis_index("grp")
     c = lax.axis_index("ctx")
@@ -71,7 +79,7 @@
         return ((z + dz + 4) % 4) * 8 + ((x + dx + 4) % 4) * 2 + yy
 
     def line(p, t, d):
-        return (0, d) if (p + t) % 2 == 0 else (d, 0)
+        return (0, d) if (p, t) in XLINE else (d, 0)
 
     def nbr(p, t, d):
         dx, dz = line(p, t, d)
@@ -183,11 +191,16 @@
         for d in (1, 3, 2):
             along(p, t, d).start()
 
+    def yget(t, a):
+        return rdma(qbuf.at[0, t, a], qbuf.at[1, t, a], *sems(1, t, a), (g, other))
+
     def send2(p, t):
         for d in range(1, 4):
             along(p, t, d).wait_recv()
         g2(p, t, 1).start()
         g2(p, t, -1).start()
+        if (p, t) in early:
+            yget(t, 0).start()
 
     def spread(p, t):
         if t < 3:
@@ -201,10 +214,19 @@
         for sign in (1, -1):
             g2(p, t, sign).wait_recv()
             g2f(p, t, sign).start()
+            if (p, t) in early:
+                yget(t, 3 if sign > 0 else 1).start()
 
     def ready(p, t):
         for sign in (1, -1):
             g2f(p, t, sign).wait_recv()
+        if (p, t) in early:
+            yget(t, 2).start()
+
+    def yready(*dists):
+        for a in dists:
+            for _, t in middle:
+                yget(t, a).wait_recv()
 
     early = [(0, 0), (0, 1)]
     middle = [(1, 0), (1, 1)]
@@ -219,8 +241,6 @@
                 cp = handed(hh, yy)
                 pl.when(jnp.logical_not(mine))(cp.start if what else cp.wait_send)
 
-    across(0).start()
-    across(1).start()
     send1(0, 0)
     send1(0, 1)
     across(2).start()
@@ -232,6 +252,13 @@
         qbuf[g % 2, 3 + g // 2, 0, 0] = qown[3]
 
     swap = rdma(cache_ref, cbuf.at[1], csem.at[3], csem.at[4], (g + 1 - 2 * k, c))
+
+    def store(ref, base, o):
+        for i in range(4):
+            ref[base + i] = o[:, 128 * i:128 * i + 128].astype(BF)
+
+    def load(ref, base):
+        return chunk([ref[base + i] for i in range(4)])
 
     nj = 2
     wj = CTX // nj
@@ -275,58 +302,38 @@
         hi = rounded(total)
         lo = total - hi
         for i, (p, t, a) in enumerate(groups):
-            obuf[p, t, a] = acc[64 * i:64 * i + 64].astype(BF).reshape(4, ROWS, LATENT)
+            for b in range(4):
+                store(obuf.at[p, t, a], TILE[b], acc[64 * i + ROWS * b:64 * i + ROWS * b + ROWS])
             tile = jnp.zeros((ROWS, 128), F32)
             for b in range(4):
                 part = slice((i * 4 + b) * ROWS, (i * 4 + b + 1) * ROWS)
                 tile = jnp.where(lane == b, top[part], tile)
                 tile = jnp.where(lane == 4 + b, hi[part], tile)
                 tile = jnp.where(lane == 8 + b, lo[part], tile)
-            stat[p, t, a] = tile.astype(BF)
+            obuf[p, t, a, STAT] = tile.astype(BF)
 
     def rsem(p, t, i):
-        n = (p * NPART + t) * 8 + i
+        n = (p * NPART + t) * 4 + i
         return rsend.at[n], rrecv.at[n]
 
     def a1(p, t, sign):
         i = 0 if sign > 0 else 1
-        half = pl.ds(0, 2) if sign > 0 else pl.ds(2, 2)
-        dev = nbr(p, t, sign)
-        return (rdma(obuf.at[p, t, 2, half], ra.at[p, t, i], *rsem(p, t, i), dev),
-                rdma(stat.at[p, t, 2], ras.at[p, t, i], *rsem(p, t, 2 + i), dev))
+        return rdma(obuf.at[p, t, 2, pl.ds(8 * i, 9)], ra.at[p, t, i], *rsem(p, t, i), nbr(p, t, sign))
 
     def a2(p, t, sign):
         i = 0 if sign > 0 else 1
-        a = 1 if sign > 0 else 3
-        dev = nbr(p, t, sign)
-        return (rdma(obuf.at[p, t, a], rc.at[p, t, i], *rsem(p, t, 4 + i), dev),
-                rdma(stat.at[p, t, a], rcs.at[p, t, i], *rsem(p, t, 6 + i), dev))
+        return rdma(obuf.at[p, t, 1 if sign > 0 else 3], rc.at[p, t, i], *rsem(p, t, 2 + i), nbr(p, t, sign))
 
     def back(p, t, d):
         dz, dx = line(p, t, d)
         if t < 3:
-            dev = (g, at(dz, dx, y if p == 0 else 1 - y))
             i = t * 7 + (d - 1 if p == 0 else 3 + d)
-            return (rdma(obuf.at[p, t, 0, d], rd.at[i], dsend.at[2 * i], drecv.at[2 * i], dev),
-                    rdma(stat.at[p, t, 0], rds.at[i], dsend.at[2 * i + 1], drecv.at[2 * i + 1], dev))
+            if p == 1 and d == 0:
+                return rdma(by.at[t], rd.at[i], dsend.at[i], drecv.at[i], (g, other))
+            return rdma(bb.at[p, t, d], rd.at[i], dsend.at[i], drecv.at[i], (g, at(dz, dx, y)))
         s = (t - 3) * 2 + p
-        dev = (s, at(dz, dx, k))
         i = (2 * h + y) * 4 + d
-        j = 2 * (s * 4 + d)
-        return (rdma(obuf.at[p, t, 0, d], rf.at[i], fsend.at[j], frecv.at[2 * i], dev),
-                rdma(stat.at[p, t, 0], rfs.at[i], fsend.at[j + 1], frecv.at[2 * i + 1], dev))
-
-    def start(pair):
-        for cp in pair:
-            cp.start()
-
-    def got(pair):
-        for cp in pair:
-            cp.wait_recv()
-
-    def gone(pair):
-        for cp in pair:
-            cp.wait_send()
+        return rdma(bb.at[p, t, d], rf.at[i], fsend.at[s * 4 + d], frecv.at[i], (s, at(dz, dx, k)))
 
     def only(pair, keep):
         return jnp.where(keep, pair[0], 4 * FLOOR), jnp.where(keep, pair[1], 0.0)
@@ -337,56 +344,66 @@
         return pltpu.roll(pair[0], 128 - b, 1), pltpu.roll(pair[1], 128 - b, 1)
 
     def begin(p, t):
-        start(a1(p, t, 1))
-        start(a1(p, t, -1))
+        a1(p, t, 1).start()
+        a1(p, t, -1).start()
 
     def r1(units):
         for p, t in units:
-            got(a1(p, t, 1))
-            got(a1(p, t, -1))
+            a1(p, t, 1).wait_recv()
+            a1(p, t, -1).wait_recv()
         for p, t in units:
             for i in range(2):
-                a = 1 if i == 0 else 3
+                own = obuf.at[p, t, 1 if i == 0 else 3]
+                came = ra.at[p, t, i]
                 inside = (lane < 2) if i == 0 else (lane >= 2) & (lane < 4)
-                top, total, (f0, f1) = combine([stats(stat[p, t, a]), only(stats(ras[p, t, i]), inside)])
-                for b in range(2):
-                    bb = 2 * i + b
-                    o = (obuf[p, t, a, bb].astype(F32) * f0[:, bb:bb + 1]
-                         + ra[p, t, i, b].astype(F32) * f1[:, bb:bb + 1])
-                    obuf[p, t, a, bb] = o.astype(BF)
-                stat[p, t, a] = packed(top, total)
-        for p, t in units:
-            start(a2(p, t, 1))
-            start(a2(p, t, -1))
+                top, total, (f0, f1) = combine([stats(own[STAT]), only(stats(came[STAT if i == 0 else 0]), inside)])
+                for b in (2 * i, 2 * i + 1):
+                    o = load(own, TILE[b]) * f0[:, b:b + 1] + load(came, TILE[b] - 8 * i) * f1[:, b:b + 1]
+                    store(own, TILE[b], o)
+                own[STAT] = packed(top, total)
+        for p, t in units:
+            a2(p, t, 1).start()
+            a2(p, t, -1).start()
 
     def r2(units):
         for p, t in units:
-            got(a2(p, t, 1))
-            got(a2(p, t, -1))
-        for p, t in units:
-            top, total, (f0, f1, f2) = combine([stats(stat[p, t, 0]), stats(rcs[p, t, 0]), stats(rcs[p, t, 1])])
+            a2(p, t, 1).wait_recv()
+            a2(p, t, -1).wait_recv()
+        for p, t in units:
+            refs = [obuf.at[p, t, 0], rc.at[p, t, 0], rc.at[p, t, 1]]
+            top, total, fs = combine([stats(r[STAT]) for r in refs])
+            tile = packed(top, total)
             for b in range(4):
-                o = (obuf[p, t, 0, b].astype(F32) * f0[:, b:b + 1] + rc[p, t, 0, b].astype(F32) * f1[:, b:b + 1]
-                     + rc[p, t, 1, b].astype(F32) * f2[:, b:b + 1])
-                obuf[p, t, 0, b] = o.astype(BF)
-            stat[p, t, 0] = packed(top, total)
+                o = load(refs[0], TILE[b]) * fs[0][:, b:b + 1]
+                for r, f in zip(refs[1:], fs[1:]):
+                    o = o + load(r, TILE[b]) * f[:, b:b + 1]
+                store(bb.at[p, t, b], 0, o)
+                bb[p, t, b, 4] = tile
         for p, t in units:
             for d in (2, 1, 3):
-                start(back(p, t, d))
-            if t < 3:
-                if p == 1:
-                    start(back(p, t, 0))
-            else:
+                back(p, t, d).start()
+            if t >= 3:
                 mine = (g == (t - 3) * 2 + p) & (y == k)
-
-                @pl.when(jnp.logical_not(mine))
-                def _():
-                    start(back(p, t, 0))
+                pl.when(jnp.logical_not(mine))(back(p, t, 0).start)
 
                 @pl.when(mine)
                 def _():
-                    rf[(2 * h + y) * 4] = obuf[p, t, 0, 0]
-                    rfs[(2 * h + y) * 4] = stat[p, t, 0]
+                    rf[(2 * h + y) * 4] = bb[p, t, 0]
+
+    def r3(units):
+        for p, t in units:
+            for d in (1, 2, 3):
+                back(p, t, d).wait_recv()
+        for p, t in units:
+            refs = [rd.at[t * 7 + 3 + d] for d in (1, 2, 3)]
+            top, total, fs = combine([stats(bb[p, t, 0, 4])] + [shifted(stats(r[4]), d + 1) for d, r in enumerate(refs)])
+            o = load(bb.at[p, t, 0], 0) * fs[0][:, 0:1]
+            for r, f in zip(refs, fs[1:]):
+                o = o + load(r, 0) * f[:, 0:1]
+            store(by.at[t], 0, o)
+            by[t, 4] = packed(top, total)
+        for p, t in units:
+            back(p, t, 0).start()
 
     att = [None] * 4
 
@@ -395,7 +412,7 @@
         top, total, fs = combine(parts)
         o = fo[t] * fs[-1][:, 0:1]
         for f, v in zip(fs[:-1], outs):
-            o = o + v.astype(F32) * f[:, 0:1]
+            o = o + load(v, 0) * f[:, 0:1]
         if last:
             att[t] = (o / total[:, 0:1]).astype(BF)
         else:
@@ -404,27 +421,26 @@
             fst[t, 1] = total
 
     def fin_half(p, t):
-        ds = (1, 2, 3) if p == 0 else (0, 1, 2, 3)
+        ds = (1, 2, 3) if p == 0 else (0,)
         for d in ds:
-            got(back(p, t, d))
+            back(p, t, d).wait_recv()
         where = [t * 7 + (d - 1 if p == 0 else 3 + d) for d in ds]
-        parts = [shifted(stats(rds[i]), d) for i, d in zip(where, ds)]
-        outs = [rd[i] for i in where]
+        parts = [shifted(stats(rd[i, 4]), d) for i, d in zip(where, ds)]
+        outs = [rd.at[i] for i in where]
         if p == 0:
-            parts.append(stats(stat[0, t, 0]))
-            outs.append(obuf[0, t, 0, 0])
+            parts.append(stats(bb[0, t, 0, 4]))
+            outs.append(bb.at[0, t, 0])
         fold_in(t, parts, outs, p == 1)
 
     def fin_slot():
         for i in range(16):
-            cps = (rdma(obuf.at[0, 3, 0, 0], rf.at[i], fsend.at[0], frecv.at[2 * i], (g, c)),
-                   rdma(stat.at[0, 3, 0], rfs.at[i], fsend.at[1], frecv.at[2 * i + 1], (g, c)))
+            cp = rdma(bb.at[0, 3, 0], rf.at[i], fsend.at[0], frecv.at[i], (g, c))
             if i % 4 == 0:
                 mine = (y == k) & (i // 4 == 2 * h + y)
-                pl.when(jnp.logical_not(mine))(functools.partial(got, cps))
+                pl.when(jnp.logical_not(mine))(cp.wait_recv)
             else:
-                got(cps)
-        fold_in(3, [shifted(stats(rfs[i]), i % 4) for i in range(16)], [rf[i] for i in range(16)], True)
+                cp.wait_recv()
+        fold_in(3, [shifted(stats(rf[i, 4]), i % 4) for i in range(16)], [rf.at[i] for i in range(16)], True)
 
     def each(f, units):
         for u in units:
@@ -434,7 +450,6 @@
         return [(p, t, a) for a in dists for p, t in units]
 
     phase("g1")
-    each(spread, middle)
     each(send2, early)
     spread(*late[0])
     each(spread, slot_u)
@@ -442,35 +457,28 @@
     phase("B1")
     attend(of(early, 0))
     phase("g2")
-    each(send2, middle)
     each(relay2, early)
     each(send2, late)
     swap.start()
     phase("B2")
     attend(of(early, 1, 3))
     phase("g3")
-    each(send2, slot_u[:2])
-    each(relay2, middle)
-    each(send2, slot_u[2:])
+    each(send2, slot_u)
     each(ready, early)
+    phase("g3y")
+    yready(0)
     phase("B3")
     attend(of(early, 2) + of(middle, 0))
     each(begin, early)
     phase("g4")
     each(relay2, late)
+    each(relay2, slot_u[:2])
+    phase("g4y")
+    yready(1, 3)
     phase("B4")
     attend(of(middle, 1, 3))
     phase("g5")
-    each(relay2, slot_u[:2])
-    each(ready, middle)
-    each(ready, late)
-    phase("B5")
-    attend(of(middle, 2) + of(late, 2))
-    each(begin, middle)
-    each(begin, late)
-    phase("g6")
     each(relay2, slot_u[2:])
-    r1(early)
     swap.wait()
 
     def slot(i):
@@ -482,37 +490,50 @@
         phase("rs%d" % i)
 
     slot(0)
+    r1(early)
+    phase("g6")
+    yready(2)
+    each(ready, late)
+    phase("B5")
+    attend(of(middle, 2) + of(late, 2))
+    each(begin, middle)
+    each(begin, late)
     slot(1)
+    r1(slot_u[0:1])
+    slot(2)
+    r2(early)
     r1(middle)
-    r2(early)
-    slot(2)
-    r1(slot_u[0:1])
     slot(3)
     r1(slot_u[1:2])
-    r2(middle)
     phase("M3")
     attend(of(late, 1, 3) + of(late[:1], 0))
     phase("rm3")
     r1(late)
+    r2(middle)
     r1(slot_u[2:3])
     r2(slot_u[0:1])
-    fin_half(0, 0)
-    fin_half(0, 1)
     phase("E")
     attend(of(late[1:], 0))
     phase("re")
     r1(slot_u[3:])
     r2(slot_u[1:2])
+    phase("rlate")
+    r2(late)
+    phase("rmid")
+    r3(middle)
+    fin_half(0, 0)
+    fin_half(0, 1)
+    phase("rs12")
+    r2(slot_u[2:3])
+    phase("rl3")
+    r3(late[:1])
+    phase("rs13")
+    r2(slot_u[3:])
+    phase("f1")
     fin_half(1, 0)
     fin_half(1, 1)
-    phase("rlate")
-    r2(late)
-    phase("rs12")
-    r2(slot_u[2:3])
-    phase("rs13")
-    r2(slot_u[3:])
+    fin_half(0, 2)
     phase("f2")
-    fin_half(0, 2)
     fin_half(1, 2)
     phase("fs")
     fin_slot()
@@ -548,19 +569,25 @@
     handed_do(False)
     for p, t in order:
         for d in (1, 2, 3):
-            along(p, t, d).wait_send()
-            gone(back(p, t, d))
+            if (p, t) not in middle:
+                along(p, t, d).wait_send()
+            back(p, t, d).wait_send()
         if t >= 3:
             mine = (g == (t - 3) * 2 + p) & (y == k)
-            pl.when(jnp.logical_not(mine))(functools.partial(gone, back(p, t, 0)))
+            pl.when(jnp.logical_not(mine))(back(p, t, 0).wait_send)
         elif p == 1:
-            across(t).wait_send()
-            gone(back(p, t, 0))
+            back(p, t, 0).wait_send()
+            if (p, t) in middle:
+                for a in range(4):
+                    yget(t, a).wait_send()
+            else:
+                across(t).wait_send()
         for sign in (1, -1):
-            g2(p, t, sign).wait_send()
-            g2f(p, t, sign).wait_send()
-            gone(a1(p, t, sign))
-            gone(a2(p, t, sign))
+            if (p, t) not in middle:
+                g2(p, t, sign).wait_send()
+                g2f(p, t, sign).wait_send()
+            a1(p, t, sign).wait_send()
+            a2(p, t, sign).wait_send()
 
     res = sbuf[c][:, :OUTW].astype(F32)
     for rel in range(1, NPEER):
@@ -592,17 +619,18 @@
             VM((2, KEYW, CTX), BF),
             VM((4, ROWS, KEYW), BF),
             VM(U + (4, 4, ROWS, KEYW), BF),
-            VM(U + (4, 4, ROWS, LATENT), BF),
-            VM(U + (4, ROWS, 128), BF),
-            VM(U + (2, 2, ROWS, LATENT), BF), VM(U + (2, ROWS, 128), BF),
-            VM(U + (2, 4, ROWS, LATENT), BF), VM(U + (2, ROWS, 128), BF),
-            VM((21, ROWS, LATENT), BF), VM((21, ROWS, 128), BF),
-            VM((16, ROWS, LATENT), BF), VM((16, ROWS, 128), BF),
+            VM(U + (4, 17, ROWS, 128), BF),
+            VM(U + (2, 9, ROWS, 128), BF),
+            VM(U + (2, 17, ROWS, 128), BF),
+            VM(U + (4, 5, ROWS, 128), BF),
+            VM((3, 5, ROWS, 128), BF),
+            VM((21, 5, ROWS, 128), BF),
+            VM((16, 5, ROWS, 128), BF),
             VM((NPEER, ROWS, 256), BF), VM((NPEER, ROWS, 256), BF),
             VM((512, 7168), BF), VM((4, LATENT, 128), BF),
             VM((4, ROWS, LATENT), F32), VM((4, 2, ROWS, 128), F32),
-            dma((5,)), dma((44,)), dma((40,)), dma((40,)), dma((40,)), dma((80,)), dma((80,)),
-            dma((NPEER,)), dma((NPEER,)), dma((42,)), dma((42,)), dma((32,)), dma((32,)),
+            dma((5,)), dma((44,)), dma((40,)), dma((40,)), dma((40,)), dma((40,)), dma((40,)),
+            dma((NPEER,)), dma((NPEER,)), dma((21,)), dma((21,)), dma((16,)), dma((16,)),
         ],
         compiler_params=pltpu.CompilerParams(collective_id=0, has_side_effects=True,
                                              vmem_limit_bytes=56 * 1024 * 1024),

time: 69.7 us -> 65.8 us (0.944); the launches traced: 68.7 us -> 65.6 us
  Pallas kernels: 67.3 us -> 64.3 us
    pallas_call x1, Pallas kernels: 67.3 us -> 64.3 us  [body(): pl.pallas_call(kernel, out_shape=jax.ShapeDtypeStruct((4, 1, 4, OUTW), BF...]
where the time goes in v4:
time: 65.8 us; the launch traced here: 65.6 us
  Pallas kernels  64.3 us (98%)
  local copies, waits for them, and re-layouts  1.3 us (2%)
    pallas_call x1, Pallas kernels, body(): pl.pallas_call(kernel, out_shape=jax.ShapeDtypeStruct((4, 1, 4, OUTW), BF...  64.3 us

profile of v4, /device:TPU:0, one launch (start us, length us, event | category | flops | bytes accessed | tf_op | source)
XLA Modules:
  0.0 65.6 jit_solution(10799030922622934140)
XLA Ops:
  0.0 64.3 %mla_step.1 = bf16[4,1,4,224]{3,2,1,0:T(4,128)(2,1)} custom-call(s32[4]{0:T(128)} %len_ref.1, s32[4]{0:T(128)} %don_ref.1, bf16[4,1,4,4,576]{4,3,2,1,0:T(4,128)(2,1)} %q_ref.1, bf16[4,1,4,576]{3,2,1,0:T(4,128)(2,1)} %nl_ref.1, bf16[576,2048]{1,0:T(8,128)(2,1)} %bitcast.3, bf16[4,512,128]{2,1,0:T(8,128)(2,1)} %vu_ref.1, bf16[512,7168]{1,0:T(8,128)(2,1)} %op_ref.1), custom_call_target="tpu_custom_call" | custom-call | tf_op jit(solution)/shard_map/mla_step/pallas_call | solution.py:613
  64.3 1.3 %copy.9 = bf16[4,1,4,224]{3,2,1,0:T(4,128)(2,1)} copy(bf16[4,1,4,224]{3,2,1,0:T(4,128)(2,1)} %mla_step.1) | data formatting | bytes 14336

commit v5 on v4

--- a/solution.py
+++ b/solution.py
@@ -328,9 +328,10 @@
         dz, dx = line(p, t, d)
         if t < 3:
             i = t * 7 + (d - 1 if p == 0 else 3 + d)
-            if p == 1 and d == 0:
+            if (p, t) in middle and d == 0:
                 return rdma(by.at[t], rd.at[i], dsend.at[i], drecv.at[i], (g, other))
-            return rdma(bb.at[p, t, d], rd.at[i], dsend.at[i], drecv.at[i], (g, at(dz, dx, y)))
+            home = y if p == 0 or (p, t) in middle else 1 - y
+            return rdma(bb.at[p, t, d], rd.at[i], dsend.at[i], drecv.at[i], (g, at(dz, dx, home)))
         s = (t - 3) * 2 + p
         i = (2 * h + y) * 4 + d
         return rdma(bb.at[p, t, d], rf.at[i], fsend.at[s * 4 + d], frecv.at[i], (s, at(dz, dx, k)))
@@ -382,6 +383,8 @@
         for p, t in units:
             for d in (2, 1, 3):
                 back(p, t, d).start()
+            if (p, t) in late[:1]:
+                back(p, t, 0).start()
             if t >= 3:
                 mine = (g == (t - 3) * 2 + p) & (y == k)
                 pl.when(jnp.logical_not(mine))(back(p, t, 0).start)
@@ -421,7 +424,7 @@
             fst[t, 1] = total
 
     def fin_half(p, t):
-        ds = (1, 2, 3) if p == 0 else (0,)
+        ds = (1, 2, 3) if p == 0 else (0,) if (p, t) in middle else (0, 1, 2, 3)
         for d in ds:
             back(p, t, d).wait_recv()
         where = [t * 7 + (d - 1 if p == 0 else 3 + d) for d in ds]
@@ -499,40 +502,38 @@
     each(begin, middle)
     each(begin, late)
     slot(1)
+    slot(2)
+    r1(middle)
     r1(slot_u[0:1])
-    slot(2)
-    r2(early)
-    r1(middle)
     slot(3)
     r1(slot_u[1:2])
     phase("M3")
-    attend(of(late, 1, 3) + of(late[:1], 0))
+    attend(of(late, 1, 3))
     phase("rm3")
     r1(late)
+    r1(slot_u[2:3])
     r2(middle)
-    r1(slot_u[2:3])
-    r2(slot_u[0:1])
     phase("E")
-    attend(of(late[1:], 0))
+    attend(of(late, 0))
     phase("re")
     r1(slot_u[3:])
-    r2(slot_u[1:2])
+    r2(slot_u[0:2])
     phase("rlate")
     r2(late)
     phase("rmid")
     r3(middle)
+    r2(early)
+    phase("rs12")
+    r2(slot_u[2:3])
+    phase("rs13")
+    r2(slot_u[3:])
+    phase("f0")
     fin_half(0, 0)
     fin_half(0, 1)
-    phase("rs12")
-    r2(slot_u[2:3])
-    phase("rl3")
-    r3(late[:1])
-    phase("rs13")
-    r2(slot_u[3:])
     phase("f1")
+    fin_half(0, 2)
     fin_half(1, 0)
     fin_half(1, 1)
-    fin_half(0, 2)
     phase("f2")
     fin_half(1, 2)
     phase("fs")
@@ -623,7 +624,7 @@
             VM(U + (2, 9, ROWS, 128), BF),
             VM(U + (2, 17, ROWS, 128), BF),
             VM(U + (4, 5, ROWS, 128), BF),
-            VM((3, 5, ROWS, 128), BF),
+            VM((2, 5, ROWS, 128), BF),
             VM((21, 5, ROWS, 128), BF),
             VM((16, 5, ROWS, 128), BF),
             VM((NPEER, ROWS, 256), BF), VM((NPEER, ROWS, 256), BF),

time: 65.8 us -> 65 us (0.988)
  Pallas kernels: 64.3 us -> 63.2 us
    pallas_call x1, Pallas kernels: 64.3 us -> 63.2 us  [body(): pl.pallas_call(kernel, out_shape=jax.ShapeDtypeStruct((4, 1, 4, OUTW), BF...]
where the time goes in v5:
time: 65 us; the launch traced here: 64.5 us
  Pallas kernels  63.2 us (97%)
  local copies, waits for them, and re-layouts  1.3 us (2%)
    pallas_call x1, Pallas kernels, body(): pl.pallas_call(kernel, out_shape=jax.ShapeDtypeStruct((4, 1, 4, OUTW), BF...  63.2 us
    unnamed x1, local copies, waits for them, and re-layouts  1.3 us

profile of v5, /device:TPU:0, one launch (start us, length us, event | category | flops | bytes accessed | tf_op | source)
XLA Modules:
  0.0 64.5 jit_solution(9070718099199376840)
XLA Ops:
  0.0 63.2 %mla_step.1 = bf16[4,1,4,224]{3,2,1,0:T(4,128)(2,1)} custom-call(s32[4]{0:T(128)} %len_ref.1, s32[4]{0:T(128)} %don_ref.1, bf16[4,1,4,4,576]{4,3,2,1,0:T(4,128)(2,1)} %q_ref.1, bf16[4,1,4,576]{3,2,1,0:T(4,128)(2,1)} %nl_ref.1, bf16[576,2048]{1,0:T(8,128)(2,1)} %bitcast.3, bf16[4,512,128]{2,1,0:T(8,128)(2,1)} %vu_ref.1, bf16[512,7168]{1,0:T(8,128)(2,1)} %op_ref.1), custom_call_target="tpu_custom_call" | custom-call | tf_op jit(solution)/shard_map/mla_step/pallas_call | solution.py:614
  63.2 1.3 %copy.9 = bf16[4,1,4,224]{3,2,1,0:T(4,128)(2,1)} copy(bf16[4,1,4,224]{3,2,1,0:T(4,128)(2,1)} %mla_step.1) | data formatting | bytes 14336

commit v6 on v5

--- a/solution.py
+++ b/solution.py
@@ -557,14 +557,19 @@
         return rdma(sbuf.at[dest], rbuf.at[rel], xsend.at[dest], xrecv.at[rel], (g, dest))
 
     width = 8 * OUTW
-    for blk in range(4):
-        term = jnp.dot(joined, opv[:, blk * width:(blk + 1) * width], preferred_element_type=F32)
+    for step in (2, 1, 3, 0):
+        blk = (z + step) % 4
+        cols = pl.ds(pl.multiple_of(blk * width, 128), width)
+        term = jnp.dot(joined, opv[:, cols], preferred_element_type=F32)
+        for i in range(8):
+            sbuf[blk * 8 + i, :, :OUTW] = term[:, i * OUTW:(i + 1) * OUTW].astype(BF)
         for i in range(8):
             dest = blk * 8 + i
-            sbuf[dest, :, :OUTW] = term[:, i * OUTW:(i + 1) * OUTW].astype(BF)
-        for i in range(8):
-            dest = blk * 8 + i
-            pl.when(dest != c)(outc(dest, (c - dest + NPEER) % NPEER).start)
+            cp = outc(dest, (c - dest + NPEER) % NPEER)
+            if step:
+                cp.start()
+            else:
+                pl.when(dest != c)(cp.start)
     phase("outx")
 
     handed_do(False)

time: 65 us -> 65.4 us (level)
  no operation moved by 1% of the time
where the time goes in v6:
time: 65.4 us; the launch traced here: 64.8 us
  Pallas kernels  63.5 us (97%)
  local copies, waits for them, and re-layouts  1.3 us (2%)
    pallas_call x1, Pallas kernels, body(): pl.pallas_call(kernel, out_shape=jax.ShapeDtypeStruct((4, 1, 4, OUTW), BF...  63.5 us

profile of v6, /device:TPU:0, one launch (start us, length us, event | category | flops | bytes accessed | tf_op | source)
XLA Modules:
  0.0 64.8 jit_solution(11652161081610438143)
XLA Ops:
  0.0 63.5 %mla_step.1 = bf16[4,1,4,224]{3,2,1,0:T(4,128)(2,1)} custom-call(s32[4]{0:T(128)} %len_ref.1, s32[4]{0:T(128)} %don_ref.1, bf16[4,1,4,4,576]{4,3,2,1,0:T(4,128)(2,1)} %q_ref.1, bf16[4,1,4,576]{3,2,1,0:T(4,128)(2,1)} %nl_ref.1, bf16[576,2048]{1,0:T(8,128)(2,1)} %bitcast.3, bf16[4,512,128]{2,1,0:T(8,128)(2,1)} %vu_ref.1, bf16[512,7168]{1,0:T(8,128)(2,1)} %op_ref.1), custom_call_target="tpu_custom_call" | custom-call | tf_op jit(solution)/shard_map/mla_step/pallas_call | solution.py:619
  63.5 1.3 %copy.9 = bf16[4,1,4,224]{3,2,1,0:T(4,128)(2,1)} copy(bf16[4,1,4,224]{3,2,1,0:T(4,128)(2,1)} %mla_step.1) | data formatting | bytes 14336
